TPU v7x, 32 devices: a whole 2x2x4 slice. The times are simulated.
32 devices in a mesh: dp: 8 (over z, y), tensor: 4 (over x, core).
Axes of the slice: x: 2, y: 2, z: 4, core: 2. Of those that a mesh axis runs over, the one named last changes fastest.
Arguments:
- qkv: bfloat16 [3, 2048, 4096], P(None, 'dp', 'tensor'), may hold values from -6 to 6
- segment_ids: int32 [8, 4, 64], P('dp'), may hold values from 0 to 1, never falling along the last dimension, each value on 1 to 63 neighbouring positions
- out_weight: bfloat16 [4096, 4096], P(None, 'tensor'), may hold values from -0.09375 to 0.09375
- out_bias: bfloat16 [4096], replicated, may hold values from -3 to 3
- upstream: bfloat16 [2048, 4096], P(('dp', 'tensor')), may hold values from -6 to 6
- pre_act: bfloat16 [2048, 8192], P('dp', 'tensor'), may hold values from -6 to 6
- down_weight: bfloat16 [4096, 8192], P('dp', 'tensor'), may hold values from -0.0625 to 0.0625
Outputs:
- attention_out: float32 [2048, 4096], P(('dp', 'tensor'))
- act_grad: float32 [2048, 8192], P('dp', 'tensor')
- weight_grad: float32 [4096, 8192], P('dp', 'tensor')
Inputs may be any that keep to these rules, and one draw needn't show every extreme that they name: `segment_ids`: within each pack the ids never fall; 2 images a pack, each of 1 to 63 tokens.
All inputs are finite; a program needn't handle non-finite values.
Results may differ from a plain program's by a relative error of at most 0.0055.
Values may be sent and summed in bfloat16 or wider, within the bound.
A program may use at most 128 MiB of HBM per device.

v0:
```python
import functools
import math

import jax
import jax.numpy as jnp
from jax import lax
from jax.experimental import pallas as pl
from jax.experimental.pallas import tpu as pltpu
from jax.sharding import PartitionSpec as P

HEAD = 128
ROWS_DEV = 64
CHUNKS = 8
LAG = 3
AHEAD = 6
EARLY = 2
HEADS_TICK = 2
SPANS_TICK = 2

root_half = 1.0 / math.sqrt(2.0)
inv_root_tau = 1.0 / math.sqrt(2.0 * math.pi)


def gelu_exact(argument):
    return 0.5 * argument * (1.0 + lax.erf(argument * root_half))


def gelu_slope(argument):
    return (
        0.5 * (1.0 + lax.erf(argument * root_half))
        + argument * jnp.exp(-0.5 * argument * argument) * inv_root_tau
    )


def kernel(
    sizes,
    qkv_hbm, segments, ow_hbm, bias, up_hbm, pre, w_hbm,
    att_out, hid_out, wg_out,
    qkv, ow, ctx, part, att_recv,
    u_all, u_t, w_all, a_all, a_own, same_ref, h_right, h_left, g_send, g_recv,
    local_sem, loc_wa, att_s, att_r,
    uz_s, uz_r, ux_s, ux_r, uc_s, uc_r,
    w_s, w_r, ar_s, ar_r, al_s, al_r,
    hr_s, hr_r, hl_s, hl_r, g_s, g_r,
):
    OUT, INN, TEN = sizes
    XS = TEN // 2
    g = lax.axis_index("dp")
    t = lax.axis_index("tensor")
    o, i = g // INN, lax.rem(g, INN)
    x, core = t // 2, lax.rem(t, 2)
    rows_w, ff = w_hbm.shape
    rows = up_hbm.shape[0]
    tokens = rows * TEN
    fc = ff // CHUNKS
    dcols = rows_w * INN
    HOPS = OUT - 1

    def remote(src, dst, ssem, rsem, dp, tensor):
        return pltpu.make_async_remote_copy(
            src_ref=src, dst_ref=dst, send_sem=ssem, recv_sem=rsem,
            device_id={"dp": dp, "tensor": tensor},
            device_id_type=pl.DeviceIdType.MESH,
        )

    def cols(c):
        return pl.ds(pl.multiple_of(c * fc, fc), fc)

    def u_rows(oo, tt):
        return u_all.at[pl.ds(pl.multiple_of((oo * TEN + tt) * rows, rows), rows), :]

    def a_rows(c, oo):
        return a_all.at[c, pl.ds(pl.multiple_of(oo * tokens, tokens), tokens), :]

    def w_rows(c, ii):
        return w_all.at[c, pl.ds(pl.multiple_of(ii * rows_w, rows_w), rows_w), :]

    def uz(j):
        to = lax.rem(o + j, OUT)
        return remote(
            up_hbm.at[:, pl.ds(pl.multiple_of(to * dcols, dcols), dcols)],
            u_rows(o, t), uz_s.at[j - 1], uz_r.at[j - 1], to * INN + i, t,
        )

    def ux(j, k):
        block = u_rows(lax.rem(o - j + OUT, OUT), t)
        return remote(block, block, ux_s.at[j, k - 1], ux_r.at[j, k - 1], g,
                      lax.rem(x + k, XS) * 2 + core)

    def uc(j, k):
        block = u_rows(lax.rem(o - j + OUT, OUT), lax.rem(x - k + XS, XS) * 2 + core)
        return remote(block, block, uc_s.at[j, k], uc_r.at[j, k], g, x * 2 + 1 - core)

    def wx(c, j):
        return remote(w_hbm.at[:, cols(c)], w_rows(c, i), w_s.at[c, j - 1], w_r.at[c, j - 1],
                      o * INN + lax.rem(i + j, INN), t)

    def a_right(c, s, own):
        dst = a_rows(c, jnp.maximum(o - s, 0))
        src = a_own.at[c] if own else dst
        return remote(src, dst, ar_s.at[c, s], ar_r.at[c, s],
                      jnp.minimum(o + 1, OUT - 1) * INN + i, t)

    def a_left(c, s, own):
        dst = a_rows(c, jnp.minimum(o + s, OUT - 1))
        src = a_own.at[c] if own else dst
        return remote(src, dst, al_s.at[c, s], al_r.at[c, s],
                      jnp.maximum(o - 1, 0) * INN + i, t)

    def h_r(c, e):
        return remote(h_right.at[c, e], h_right.at[c, e], hr_s.at[c, e], hr_r.at[c, e],
                      jnp.minimum(o + 1, OUT - 1) * INN + i, t)

    def h_l(c, e):
        return remote(h_left.at[c, e], h_left.at[c, e], hl_s.at[c, e], hl_r.at[c, e],
                      jnp.maximum(o - 1, 0) * INN + i, t)

    def gx(c, j):
        return remote(g_send.at[c, j - 1], g_recv.at[c, j - 1], g_s.at[c, j - 1], g_r.at[c, j - 1],
                      o * INN + lax.rem(i + j, INN), t)

    def att(j):
        to = lax.rem(t + j, TEN)
        return remote(part.at[pl.ds(pl.multiple_of(to * rows, rows), rows), :],
                      att_recv.at[j - 1], att_s.at[j - 1], att_r.at[j - 1], g, to)

    def own_w(c):
        return pltpu.make_async_copy(w_hbm.at[:, cols(c)], w_rows(c, i), loc_wa.at[0, c])

    def loop(count, fn):
        def step(index, carry):
            fn(index)
            return carry
        lax.fori_loop(0, count, step, 0)

    own_u = pltpu.make_async_copy(
        up_hbm.at[:, pl.ds(pl.multiple_of(o * dcols, dcols), dcols)], u_rows(o, t), local_sem.at[0])
    load_qkv = pltpu.make_async_copy(qkv_hbm, qkv, local_sem.at[1])
    load_ow = pltpu.make_async_copy(ow_hbm, ow, local_sem.at[2])

    own_u.start()
    for j in range(1, OUT):
        uz(j).start()
    load_qkv.start()

    def a_tick(k):
        for s in range(OUT):
            n = k - s * LAG
            if isinstance(k, int):
                if n >= 0 and n % HOPS == 0 and n // HOPS < CHUNKS:
                    a_step(n // HOPS, s)
            else:
                @pl.when((n >= 0) & (lax.rem(n, HOPS) == 0) & (n < CHUNKS * HOPS))
                def _():
                    a_step(n // HOPS, s)

    def a_step(c, s):
        @pl.when(o >= s)
        def _():
            if s:
                got = a_rows(c, o - s)
                remote(got, got, ar_s.at[c, s - 1], ar_r.at[c, s - 1], g, t).wait_recv()
            if s < HOPS:
                @pl.when(o < OUT - 1)
                def _():
                    a_right(c, s, s == 0).start()

        @pl.when(o + s <= OUT - 1)
        def _():
            if s:
                got = a_rows(c, o + s)
                remote(got, got, al_s.at[c, s - 1], al_r.at[c, s - 1], g, t).wait_recv()
            if s < HOPS:
                @pl.when(o > 0)
                def _():
                    a_left(c, s, s == 0).start()

    def start_w(c):
        for j in range(1, INN):
            wx(c, j).start()
        own_w(c).start()

    loop(CHUNKS, start_w)
    load_ow.start()

    def activate(c):
        act = gelu_exact(pre[:, cols(c)].astype(jnp.float32)).astype(jnp.bfloat16)
        a_own[c] = act
        a_all[c, pl.ds(pl.multiple_of(o * tokens, tokens), tokens), :] = act

    loop(min(EARLY, CHUNKS), activate)
    for k in range(AHEAD):
        a_tick(k)
    own_u.wait()
    for k in range(1, XS):
        ux(0, k).start()
    uc(0, 0).start()

    for j in range(1, OUT):
        uz(j).wait_recv()
        for k in range(1, XS):
            ux(j, k).start()
        uc(j, 0).start()
    loop(CHUNKS - min(EARLY, CHUNKS), lambda c: activate(c + EARLY))
    load_qkv.wait()
    load_ow.wait()
    for j in range(OUT):
        for k in range(1, XS):
            ux(j, k).wait_recv()
            uc(j, k).start()
    for j in range(OUT):
        for k in range(XS):
            uc(j, k).wait_recv()

    heads = qkv.shape[2] // HEAD
    block = min(tokens, 4 * ROWS_DEV)
    scale = 1.0 / math.sqrt(HEAD)

    labels = segments[0].astype(jnp.float32)
    packs, length = labels.shape
    spread = (
        lax.rem(lax.broadcasted_iota(jnp.int32, (length, tokens), 1), length)
        == lax.broadcasted_iota(jnp.int32, (length, tokens), 0)
    ).astype(jnp.float32)
    wide = jnp.dot(labels, spread, preferred_element_type=jnp.float32)
    pack = lax.broadcasted_iota(jnp.int32, (packs, tokens), 0)
    here = lax.broadcasted_iota(jnp.int32, (packs, tokens), 1) // length == pack
    name = jnp.sum(
        jnp.where(here, wide + 2.0 * pack.astype(jnp.float32), 0.0), axis=0, keepdims=True)
    for b in range(tokens // block):
        across = jnp.broadcast_to(name[:, b * block : (b + 1) * block], (block, block))
        same_ref[b] = (across == across.T).astype(jnp.float32)

    def head(h):
        lanes = pl.ds(pl.multiple_of(h * HEAD, HEAD), HEAD)
        for b in range(tokens // block):
            mine = slice(b * block, (b + 1) * block)
            same = same_ref[b] > 0.5
            scores = lax.dot_general(
                qkv[0, mine, lanes], qkv[1, mine, lanes], (((1,), (1,)), ((), ())),
                preferred_element_type=jnp.float32) * scale
            masked = jnp.where(same, scores, -1e30)
            top = jnp.max(masked, axis=1, keepdims=True)
            exponent = jnp.where(same, jnp.exp(masked - top), 0.0)
            weights = (exponent / jnp.sum(exponent, axis=1, keepdims=True)).astype(jnp.bfloat16)
            ctx[mine, lanes] = jnp.dot(
                weights, qkv[2, mine, lanes], preferred_element_type=jnp.float32
            ).astype(jnp.bfloat16)

    nb = 512
    spans = ow.shape[0] // nb

    def project(n):
        span = pl.ds(pl.multiple_of(n * nb, nb), nb)
        part[:, span] = lax.dot_general(
            ctx[...], ow[span, :], (((1,), (1,)), ((), ())),
            preferred_element_type=jnp.float32).astype(jnp.bfloat16)

    def flip(e):
        span = pl.ds(pl.multiple_of(e * tokens, tokens), tokens)
        u_t[:, span] = u_all[span, :].T

    def partial(c, e):
        span = pl.ds(pl.multiple_of(e * tokens, tokens), tokens)
        return jnp.dot(u_all[span, :], w_all[c], preferred_element_type=jnp.float32)

    def h_tick(n, e_of, held, copy, sends, first):
        @pl.when((n >= 0) & (n < CHUNKS * HOPS))
        def _():
            c, e = n // HOPS, e_of(lax.rem(n, HOPS))

            @pl.when(sends(e) & first)
            def _():
                held[c, e] = partial(c, e).astype(jnp.bfloat16)
                copy(c, e).start()

            @pl.when(sends(e) & jnp.logical_not(first))
            def _():
                mine = partial(c, e)
                copy(c, e).wait_recv()
                held[c, e] = (mine + held[c, e].astype(jnp.float32)).astype(jnp.bfloat16)
                copy(c, e).start()

    def weight_chunk(c):
        for j in range(1, INN):
            to = lax.rem(i + j, INN)
            span = pl.ds(pl.multiple_of(to * rows_w, rows_w), rows_w)
            g_send[c, j - 1] = jnp.dot(
                u_t[span, :], a_all[c], preferred_element_type=jnp.float32).astype(jnp.bfloat16)
            gx(c, j).start()
        span = pl.ds(pl.multiple_of(i * rows_w, rows_w), rows_w)
        wg_out[:, cols(c)] = jnp.dot(
            u_t[span, :], a_all[c], preferred_element_type=jnp.float32)

    head_ticks = -(-heads // HEADS_TICK)
    span_ticks = -(-spans // SPANS_TICK)

    def tick(k):
        c0 = k // HOPS

        @pl.when((lax.rem(k, HOPS) == 0) & (c0 < CHUNKS))
        def _():
            own_w(c0).wait()
            for j in range(1, INN):
                wx(c0, j).wait_recv()

        h_tick(k - LAG * o, lambda s: OUT - 1 - s, h_right, h_r, lambda e: o < e, o == 0)
        h_tick(k - LAG * (OUT - 1 - o), lambda s: s, h_left, h_l, lambda e: o > e, o == OUT - 1)

        a_tick(k + AHEAD)

        @pl.when((lax.rem(k, HOPS) == 0) & (c0 < CHUNKS))
        def _():
            hid_out[:, cols(c0)] = partial(c0, o)

        @pl.when(k == 0)
        def _():
            loop(OUT, flip)

        ka = k + AHEAD - HOPS * LAG
        ca = ka // HOPS

        @pl.when((ka >= 0) & (lax.rem(ka, HOPS) == 0) & (ca < CHUNKS))
        def _():
            weight_chunk(ca)

        @pl.when(k < head_ticks)
        def _():
            for r in range(HEADS_TICK):
                head(jnp.minimum(k * HEADS_TICK + r, heads - 1))

        kp = k - head_ticks

        @pl.when((kp >= 0) & (kp < span_ticks))
        def _():
            for r in range(SPANS_TICK):
                project(jnp.minimum(kp * SPANS_TICK + r, spans - 1))

        @pl.when(kp == span_ticks)
        def _():
            for j in range(1, TEN):
                att(j).start()

        cf = c0 - LAG

        @pl.when((lax.rem(k, HOPS) == 0) & (cf >= 0))
        def _():
            @pl.when(o > 0)
            def _():
                h_r(cf, o).wait_recv()
                hid_out[:, cols(cf)] += h_right[cf, o].astype(jnp.float32)

            @pl.when(o < OUT - 1)
            def _():
                h_l(cf, o).wait_recv()
                hid_out[:, cols(cf)] += h_left[cf, o].astype(jnp.float32)

            hid_out[:, cols(cf)] *= gelu_slope(pre[:, cols(cf)].astype(jnp.float32))

    loop((CHUNKS + LAG) * HOPS, tick)

    total = part[pl.ds(pl.multiple_of(t * rows, rows), rows), :].astype(jnp.float32)
    total = total + bias[...].astype(jnp.float32)[None, :]
    for j in range(1, TEN):
        att(j).wait_recv()
        total = total + att_recv[j - 1].astype(jnp.float32)
    att_out[...] = total

    factor = 1.0 / (OUT * INN)

    def finish(c):
        acc = wg_out[:, cols(c)]
        for j in range(1, INN):
            gx(c, j).wait_recv()
            acc = acc + g_recv[c, j - 1].astype(jnp.float32)
        wg_out[:, cols(c)] = acc * factor

    loop(CHUNKS, finish)

    for j in range(1, OUT):
        uz(j).wait_send()
    for j in range(OUT):
        for k in range(1, XS):
            ux(j, k).wait_send()
        for k in range(XS):
            uc(j, k).wait_send()
    for j in range(1, TEN):
        att(j).wait_send()

    def drain(c):
        for j in range(1, INN):
            wx(c, j).wait_send()
            gx(c, j).wait_send()
        for s in range(OUT - 1):
            er, el = OUT - 1 - s, s

            @pl.when(o < er)
            def _():
                h_r(c, er).wait_send()

            @pl.when(o > el)
            def _():
                h_l(c, el).wait_send()

            @pl.when((o < OUT - 1) & (o >= s))
            def _():
                a_right(c, s, s == 0).wait_send()

            @pl.when((o > 0) & (o + s <= OUT - 1))
            def _():
                a_left(c, s, s == 0).wait_send()

    loop(CHUNKS, drain)


def body(sizes, qkv, segment_ids, out_weight, out_bias, upstream, pre_act, down_weight):
    OUT, INN, TEN = sizes
    rows, width = upstream.shape
    tokens, ff = pre_act.shape
    rows_w = down_weight.shape[0]
    fc = ff // CHUNKS
    bf, f32 = jnp.bfloat16, jnp.float32
    vmem = pl.BlockSpec(memory_space=pltpu.VMEM)
    anym = pl.BlockSpec(memory_space=pl.ANY)
    dma = lambda *shape: pltpu.SemaphoreType.DMA(shape)
    block = min(tokens, 4 * ROWS_DEV)
    attention_out, act_grad, weight_grad = pl.pallas_call(
        functools.partial(kernel, sizes),
        out_shape=(
            jax.ShapeDtypeStruct((rows, width), f32),
            jax.ShapeDtypeStruct((tokens, ff), f32),
            jax.ShapeDtypeStruct((rows_w, ff), f32),
        ),
        in_specs=[anym, vmem, anym, vmem, anym, vmem, anym],
        out_specs=(vmem, vmem, vmem),
        scratch_shapes=[
            pltpu.VMEM(qkv.shape, bf),
            pltpu.VMEM(out_weight.shape, bf),
            pltpu.VMEM((tokens, qkv.shape[2]), bf),
            pltpu.VMEM((tokens, width), bf),
            pltpu.VMEM((TEN - 1, rows, width), bf),
            pltpu.VMEM((OUT * tokens, INN * rows_w), bf),
            pltpu.VMEM((INN * rows_w, OUT * tokens), bf),
            pltpu.VMEM((CHUNKS, INN * rows_w, fc), bf),
            pltpu.VMEM((CHUNKS, OUT * tokens, fc), bf),
            pltpu.VMEM((CHUNKS, tokens, fc), bf),
            pltpu.VMEM((tokens // block, block, block), f32),
            pltpu.VMEM((CHUNKS, OUT, tokens, fc), bf),
            pltpu.VMEM((CHUNKS, OUT, tokens, fc), bf),
            pltpu.VMEM((CHUNKS, INN - 1, rows_w, fc), bf),
            pltpu.VMEM((CHUNKS, INN - 1, rows_w, fc), bf),
            dma(3), dma(1, CHUNKS), dma(TEN - 1), dma(TEN - 1),
            dma(OUT - 1), dma(OUT - 1),
            dma(OUT, max(TEN // 2 - 1, 1)), dma(OUT, max(TEN // 2 - 1, 1)),
            dma(OUT, TEN // 2), dma(OUT, TEN // 2),
            dma(CHUNKS, INN - 1), dma(CHUNKS, INN - 1),
            dma(CHUNKS, OUT - 1), dma(CHUNKS, OUT - 1),
            dma(CHUNKS, OUT - 1), dma(CHUNKS, OUT - 1),
            dma(CHUNKS, OUT), dma(CHUNKS, OUT),
            dma(CHUNKS, OUT), dma(CHUNKS, OUT),
            dma(CHUNKS, INN - 1), dma(CHUNKS, INN - 1),
        ],
        compiler_params=pltpu.CompilerParams(
            has_side_effects=True, vmem_limit_bytes=64_000_000),
        name="layer",
    )(qkv, segment_ids, out_weight, out_bias, upstream, pre_act, down_weight)
    return (attention_out, act_grad, weight_grad)


def solution(mesh):
    dp, tensor = mesh.shape["dp"], mesh.shape["tensor"]
    inner = 2 ** ((dp.bit_length() - 1) // 2)
    return jax.shard_map(
        functools.partial(body, (dp // inner, inner, tensor)),
        mesh=mesh,
        in_specs=(
            P(None, "dp", "tensor"),
            P("dp", None, None),
            P(None, "tensor"),
            P(),
            P(("dp", "tensor"), None),
            P("dp", "tensor"),
            P("dp", "tensor"),
        ),
        out_specs=(P(("dp", "tensor"), None), P("dp", "tensor"), P("dp", "tensor")),
        check_vma=False,
    )
```

profile of v0, /device:TPU:1, one launch (start us, length us, event | category | flops | bytes accessed | tf_op | source)
XLA Modules:
  0.0 141.6 jit_solution(17337831195810209202)
XLA Ops:
  0.6 133.5 %layer.1 = (f32[64,4096]{1,0:T(8,128)}, f32[256,2048]{1,0:T(8,128)}, f32[512,2048]{1,0:T(8,128)}) custom-call(bf16[3,256,1024]{2,1,0:T(8,128)(2,1)} %qkv_hbm.1, s32[1,4,64]{2,1,0:T(4,128)} %segments.1, bf16[4096,1024]{1,0:T(8,128)(2,1)} %ow_hbm.1, bf16[4096]{0:T(1024)(128)(2,1)} %bias.1, bf16[64,4096]{1,0:T(8,128)(2,1)} %up_hbm.1, bf16[256,2048]{1,0:T(8,128)(2,1)} %pre.1, ...), custom_call_target="tpu_custom_call" | custom-call | tf_op jit(solution)/shard_map/layer/pallas_call | solution.py:427
  134.2 0.0 copy-start.1
  134.2 2.4 %copy.13 = f32[64,4096]{1,0:T(8,128)} copy(f32[64,4096]{1,0:T(8,128)} %get-tuple-element.6) | data formatting | bytes 2097152
  136.6 0.0 copy-done.1
  136.6 0.0 copy-start
  136.6 1.3 copy.14
  137.9 1.6 %copy-done = f32[512,2048]{1,0:T(8,128)S(1)} copy-done((f32[512,2048]{1,0:T(8,128)S(1)}, f32[512,2048]{1,0:T(8,128)}, u32[]{:S(2)}) %copy-start) | copy-done | bytes 4194328
  139.6 2.0 %copy.15 = f32[512,2048]{1,0:T(8,128)} copy(f32[512,2048]{1,0:T(8,128)S(1)} %copy-done) | data formatting | bytes 8388608
Async XLA Ops:
  134.2 2.4 %copy-start.1 = (f32[256,2048]{1,0:T(8,128)S(1)}, f32[256,2048]{1,0:T(8,128)}, u32[]{:S(2)}) copy-start(f32[256,2048]{1,0:T(8,128)} %get-tuple-element.7) | copy-start | bytes 6291460
  136.6 2.9 %copy-start = (f32[512,2048]{1,0:T(8,128)S(1)}, f32[512,2048]{1,0:T(8,128)}, u32[]{:S(2)}) copy-start(f32[512,2048]{1,0:T(8,128)} %get-tuple-element.8) | copy-start | bytes 12582916
where the time goes:
time: 142 us
  Pallas kernels  134 us (94%)
  local copies, waits for them, and re-layouts  7.38 us (5%)
    pallas_call x1, Pallas kernels, body(): pl.pallas_call(functools.partial(kernel, sizes), out_shape=(jax.ShapeDtyp...  134 us
    unnamed x7, local copies, waits for them, and re-layouts  7.38 us

commit v1 on v0

--- a/solution.py
+++ b/solution.py
@@ -16,6 +16,7 @@
 EARLY = 2
 HEADS_TICK = 2
 SPANS_TICK = 2
+PIECES = 4
 
 root_half = 1.0 / math.sqrt(2.0)
 inv_root_tau = 1.0 / math.sqrt(2.0 * math.pi)
@@ -413,6 +414,19 @@
     loop(CHUNKS, drain)
 
 
+def write_out(att, hid, wg, att_hbm, hid_hbm, wg_hbm, sem):
+    copies = []
+    for n, (src, dst) in enumerate(((att, att_hbm), (hid, hid_hbm), (wg, wg_hbm))):
+        step = src.shape[0] // PIECES
+        for p in range(PIECES):
+            span = pl.ds(p * step, step)
+            copies.append(pltpu.make_async_copy(src.at[span, :], dst.at[span, :], sem.at[n, p]))
+    for copy in copies:
+        copy.start()
+    for copy in copies:
+        copy.wait()
+
+
 def body(sizes, qkv, segment_ids, out_weight, out_bias, upstream, pre_act, down_weight):
     OUT, INN, TEN = sizes
     rows, width = upstream.shape
@@ -424,12 +438,13 @@
     anym = pl.BlockSpec(memory_space=pl.ANY)
     dma = lambda *shape: pltpu.SemaphoreType.DMA(shape)
     block = min(tokens, 4 * ROWS_DEV)
+    held = 4 * (rows * width + tokens * ff + rows_w * ff)
     attention_out, act_grad, weight_grad = pl.pallas_call(
         functools.partial(kernel, sizes),
         out_shape=(
-            jax.ShapeDtypeStruct((rows, width), f32),
-            jax.ShapeDtypeStruct((tokens, ff), f32),
-            jax.ShapeDtypeStruct((rows_w, ff), f32),
+            pltpu.VMEM((rows, width), f32),
+            pltpu.VMEM((tokens, ff), f32),
+            pltpu.VMEM((rows_w, ff), f32),
         ),
         in_specs=[anym, vmem, anym, vmem, anym, vmem, anym],
         out_specs=(vmem, vmem, vmem),
@@ -461,10 +476,21 @@
             dma(CHUNKS, INN - 1), dma(CHUNKS, INN - 1),
         ],
         compiler_params=pltpu.CompilerParams(
-            has_side_effects=True, vmem_limit_bytes=64_000_000),
+            has_side_effects=True, vmem_limit_bytes=64_000_000 - held),
         name="layer",
     )(qkv, segment_ids, out_weight, out_bias, upstream, pre_act, down_weight)
-    return (attention_out, act_grad, weight_grad)
+    results = tuple(
+        pltpu.with_memory_space_constraint(r, pltpu.VMEM)
+        for r in (attention_out, act_grad, weight_grad))
+    return pl.pallas_call(
+        write_out,
+        out_shape=tuple(jax.ShapeDtypeStruct(r.shape, f32) for r in results),
+        in_specs=[vmem] * 3,
+        out_specs=(anym,) * 3,
+        scratch_shapes=[dma(3, PIECES)],
+        compiler_params=pltpu.CompilerParams(vmem_limit_bytes=2**20),
+        name="write_out",
+    )(*results)
 
 
 def solution(mesh):

time: 142 us -> 135 us (0.951)
  local copies, waits for them, and re-layouts: 7.38 us -> 0 us
    unnamed x7 -> x0, local copies, waits for them, and re-layouts: 7.38 us -> none
    pallas_call x1 -> x2, Pallas kernels: 134 us -> 134 us  [the longest x1 131 us: body(): pl.pallas_call(functools.partial(kernel, sizes), out_shape=(pltpu.VMEM((r...]
where the time goes in v1:
time: 135 us; the launch traced here: 134 us
  Pallas kernels  134 us (99%)
    pallas_call x1, Pallas kernels, body(): pl.pallas_call(functools.partial(kernel, sizes), out_shape=(pltpu.VMEM((r...  131 us
    pallas_call x1, Pallas kernels, body(): pl.pallas_call(write_out, out_shape=tuple((jax.ShapeDtypeStruct(r.shape,...  3.09 us

profile of v1, /device:TPU:1, one launch (start us, length us, event | category | flops | bytes accessed | tf_op | source)
XLA Modules:
  0.0 134.4 jit_solution(14018938989457425944)
XLA Ops:
  0.6 130.7 %layer.1 = (f32[64,4096]{1,0:T(8,128)S(1)}, f32[256,2048]{1,0:T(8,128)S(1)}, f32[512,2048]{1,0:T(8,128)S(1)}) custom-call(bf16[3,256,1024]{2,1,0:T(8,128)(2,1)} %qkv_hbm.1, s32[1,4,64]{2,1,0:T(4,128)} %segments.1, bf16[4096,1024]{1,0:T(8,128)(2,1)} %ow_hbm.1, bf16[4096]{0:T(1024)(128)(2,1)} %bias.1, bf16[64,4096]{1,0:T(8,128)(2,1)} %up_hbm.1, ...), custom_call_target="tpu_custom_call" | custom-call | tf_op jit(solution)/shard_map/layer/pallas_call | solution.py:442
  131.3 3.1 %write_out.1 = (f32[64,4096]{1,0:T(8,128)}, f32[256,2048]{1,0:T(8,128)}, f32[512,2048]{1,0:T(8,128)}) custom-call(f32[64,4096]{1,0:T(8,128)S(1)} %get-tuple-element.6.att, f32[256,2048]{1,0:T(8,128)S(1)} %get-tuple-element.7.hid, f32[512,2048]{1,0:T(8,128)S(1)} %get-tuple-element.8.wg), custom_call_target="tpu_custom_call" | custom-call | tf_op jit(solution)/shard_map/write_out/pallas_call | solution.py:485

commit v2 on v1

--- a/solution.py
+++ b/solution.py
@@ -11,11 +11,8 @@
 HEAD = 128
 ROWS_DEV = 64
 CHUNKS = 8
-LAG = 3
-AHEAD = 6
-EARLY = 2
-HEADS_TICK = 2
-SPANS_TICK = 2
+GROUP = 4
+DELAY = 2
 PIECES = 4
 
 root_half = 1.0 / math.sqrt(2.0)
@@ -35,10 +32,10 @@
 
 def kernel(
     sizes,
-    qkv_hbm, segments, ow_hbm, bias, up_hbm, pre, w_hbm,
+    qkv_hbm, segments, ow_hbm, bias, up_hbm, pre_hbm, w_hbm,
     att_out, hid_out, wg_out,
     qkv, ow, ctx, part, att_recv,
-    u_all, u_t, w_all, a_all, a_own, same_ref, h_right, h_left, g_send, g_recv,
+    u_all, u_t, w_all, a_all, pre, same_ref, h_right, h_left, g_send, g_recv,
     local_sem, loc_wa, att_s, att_r,
     uz_s, uz_r, ux_s, ux_r, uc_s, uc_r,
     w_s, w_r, ar_s, ar_r, al_s, al_r,
@@ -96,16 +93,14 @@
         return remote(w_hbm.at[:, cols(c)], w_rows(c, i), w_s.at[c, j - 1], w_r.at[c, j - 1],
                       o * INN + lax.rem(i + j, INN), t)
 
-    def a_right(c, s, own):
-        dst = a_rows(c, jnp.maximum(o - s, 0))
-        src = a_own.at[c] if own else dst
-        return remote(src, dst, ar_s.at[c, s], ar_r.at[c, s],
+    def a_right(c, s):
+        block = a_rows(c, jnp.maximum(o - s, 0))
+        return remote(block, block, ar_s.at[c, s], ar_r.at[c, s],
                       jnp.minimum(o + 1, OUT - 1) * INN + i, t)
 
-    def a_left(c, s, own):
-        dst = a_rows(c, jnp.minimum(o + s, OUT - 1))
-        src = a_own.at[c] if own else dst
-        return remote(src, dst, al_s.at[c, s], al_r.at[c, s],
+    def a_left(c, s):
+        block = a_rows(c, jnp.minimum(o + s, OUT - 1))
+        return remote(block, block, al_s.at[c, s], al_r.at[c, s],
                       jnp.maximum(o - 1, 0) * INN + i, t)
 
     def h_r(c, e):
@@ -139,42 +134,12 @@
     load_qkv = pltpu.make_async_copy(qkv_hbm, qkv, local_sem.at[1])
     load_ow = pltpu.make_async_copy(ow_hbm, ow, local_sem.at[2])
 
-    own_u.start()
+    load_pre = pltpu.make_async_copy(pre_hbm, pre, local_sem.at[3])
+
     for j in range(1, OUT):
         uz(j).start()
-    load_qkv.start()
-
-    def a_tick(k):
-        for s in range(OUT):
-            n = k - s * LAG
-            if isinstance(k, int):
-                if n >= 0 and n % HOPS == 0 and n // HOPS < CHUNKS:
-                    a_step(n // HOPS, s)
-            else:
-                @pl.when((n >= 0) & (lax.rem(n, HOPS) == 0) & (n < CHUNKS * HOPS))
-                def _():
-                    a_step(n // HOPS, s)
-
-    def a_step(c, s):
-        @pl.when(o >= s)
-        def _():
-            if s:
-                got = a_rows(c, o - s)
-                remote(got, got, ar_s.at[c, s - 1], ar_r.at[c, s - 1], g, t).wait_recv()
-            if s < HOPS:
-                @pl.when(o < OUT - 1)
-                def _():
-                    a_right(c, s, s == 0).start()
-
-        @pl.when(o + s <= OUT - 1)
-        def _():
-            if s:
-                got = a_rows(c, o + s)
-                remote(got, got, al_s.at[c, s - 1], al_r.at[c, s - 1], g, t).wait_recv()
-            if s < HOPS:
-                @pl.when(o > 0)
-                def _():
-                    a_left(c, s, s == 0).start()
+    load_pre.start()
+    own_u.start()
 
     def start_w(c):
         for j in range(1, INN):
@@ -182,36 +147,47 @@
         own_w(c).start()
 
     loop(CHUNKS, start_w)
+    load_qkv.start()
     load_ow.start()
+
+    right = (o, lambda p: p, a_right, ar_r, h_right, h_r)
+    left = (OUT - 1 - o, lambda p: OUT - 1 - p, a_left, al_r, h_left, h_l)
+
+    def a_wait(direction, c, s):
+        r, place, _, arrived, _, _ = direction
+        got = a_rows(c, place(jnp.maximum(r - s, 0)))
+        remote(got, got, arrived.at[c, s - 1], arrived.at[c, s - 1], g, t).wait_recv()
+
+    def a_item(direction, n):
+        r, _, copy, _, _, _ = direction
+        turn = (r + 1) * GROUP
+        rest = lax.rem(n, turn)
+        s = rest // GROUP
+        c = n // turn * GROUP + lax.rem(rest, GROUP)
+
+        @pl.when((r < OUT - 1) & (n < (r + 1) * CHUNKS))
+        def _():
+            @pl.when(s > 0)
+            def _():
+                a_wait(direction, c, s)
+            copy(c, s).start()
 
     def activate(c):
         act = gelu_exact(pre[:, cols(c)].astype(jnp.float32)).astype(jnp.bfloat16)
-        a_own[c] = act
         a_all[c, pl.ds(pl.multiple_of(o * tokens, tokens), tokens), :] = act
 
-    loop(min(EARLY, CHUNKS), activate)
-    for k in range(AHEAD):
-        a_tick(k)
+    def open_group(n):
+        activate(n)
+        a_item(right, n)
+        a_item(left, n)
+
+    load_pre.wait()
+    loop(GROUP, open_group)
     own_u.wait()
     for k in range(1, XS):
         ux(0, k).start()
     uc(0, 0).start()
-
-    for j in range(1, OUT):
-        uz(j).wait_recv()
-        for k in range(1, XS):
-            ux(j, k).start()
-        uc(j, 0).start()
-    loop(CHUNKS - min(EARLY, CHUNKS), lambda c: activate(c + EARLY))
-    load_qkv.wait()
-    load_ow.wait()
-    for j in range(OUT):
-        for k in range(1, XS):
-            ux(j, k).wait_recv()
-            uc(j, k).start()
-    for j in range(OUT):
-        for k in range(XS):
-            uc(j, k).wait_recv()
+    loop(CHUNKS - GROUP, lambda n: activate(n + GROUP))
 
     heads = qkv.shape[2] // HEAD
     block = min(tokens, 4 * ROWS_DEV)
@@ -265,24 +241,30 @@
         span = pl.ds(pl.multiple_of(e * tokens, tokens), tokens)
         return jnp.dot(u_all[span, :], w_all[c], preferred_element_type=jnp.float32)
 
-    def h_tick(n, e_of, held, copy, sends, first):
-        @pl.when((n >= 0) & (n < CHUNKS * HOPS))
-        def _():
-            c, e = n // HOPS, e_of(lax.rem(n, HOPS))
-
-            @pl.when(sends(e) & first)
-            def _():
-                held[c, e] = partial(c, e).astype(jnp.bfloat16)
-                copy(c, e).start()
-
-            @pl.when(sends(e) & jnp.logical_not(first))
-            def _():
-                mine = partial(c, e)
-                copy(c, e).wait_recv()
-                held[c, e] = (mine + held[c, e].astype(jnp.float32)).astype(jnp.bfloat16)
-                copy(c, e).start()
+    def h_item(direction, n):
+        r, place, _, _, held, copy = direction
+        m = n - (r + 1) * CHUNKS
+        e = place(OUT - 1 - m // CHUNKS)
+        c = lax.rem(m, CHUNKS)
+
+        @pl.when((m >= 0) & (r == 0))
+        def _():
+            held[c, e] = partial(c, e).astype(jnp.bfloat16)
+            copy(c, e).start()
+
+        @pl.when((m >= 0) & (r > 0) & (r < OUT - 1))
+        def _():
+            mine = partial(c, e)
+            copy(c, e).wait_recv()
+            held[c, e] = (mine + held[c, e].astype(jnp.float32)).astype(jnp.bfloat16)
+            copy(c, e).start()
 
     def weight_chunk(c):
+        for direction in (right, left):
+            @pl.when(direction[0] == OUT - 1)
+            def _():
+                for s in range(1, OUT):
+                    a_wait(direction, c, s)
         for j in range(1, INN):
             to = lax.rem(i + j, INN)
             span = pl.ds(pl.multiple_of(to * rows_w, rows_w), rows_w)
@@ -293,72 +275,60 @@
         wg_out[:, cols(c)] = jnp.dot(
             u_t[span, :], a_all[c], preferred_element_type=jnp.float32)
 
-    head_ticks = -(-heads // HEADS_TICK)
-    span_ticks = -(-spans // SPANS_TICK)
+    load_qkv.wait()
+    loop(heads, head)
+
+    for j in range(1, OUT):
+        uz(j).wait_recv()
+        for k in range(1, XS):
+            ux(j, k).start()
+        uc(j, 0).start()
+    for j in range(OUT):
+        for k in range(1, XS):
+            ux(j, k).wait_recv()
+            uc(j, k).start()
+    for j in range(OUT):
+        for k in range(XS):
+            uc(j, k).wait_recv()
+    loop(OUT, flip)
+    load_ow.wait()
 
     def tick(k):
-        c0 = k // HOPS
-
-        @pl.when((lax.rem(k, HOPS) == 0) & (c0 < CHUNKS))
-        def _():
-            own_w(c0).wait()
+        n = k + GROUP
+        first = n - CHUNKS
+
+        @pl.when((first >= 0) & (first < CHUNKS))
+        def _():
+            own_w(first).wait()
             for j in range(1, INN):
-                wx(c0, j).wait_recv()
-
-        h_tick(k - LAG * o, lambda s: OUT - 1 - s, h_right, h_r, lambda e: o < e, o == 0)
-        h_tick(k - LAG * (OUT - 1 - o), lambda s: s, h_left, h_l, lambda e: o > e, o == OUT - 1)
-
-        a_tick(k + AHEAD)
-
-        @pl.when((lax.rem(k, HOPS) == 0) & (c0 < CHUNKS))
-        def _():
-            hid_out[:, cols(c0)] = partial(c0, o)
-
-        @pl.when(k == 0)
-        def _():
-            loop(OUT, flip)
-
-        ka = k + AHEAD - HOPS * LAG
-        ca = ka // HOPS
-
-        @pl.when((ka >= 0) & (lax.rem(ka, HOPS) == 0) & (ca < CHUNKS))
-        def _():
-            weight_chunk(ca)
-
-        @pl.when(k < head_ticks)
-        def _():
-            for r in range(HEADS_TICK):
-                head(jnp.minimum(k * HEADS_TICK + r, heads - 1))
-
-        kp = k - head_ticks
-
-        @pl.when((kp >= 0) & (kp < span_ticks))
-        def _():
-            for r in range(SPANS_TICK):
-                project(jnp.minimum(kp * SPANS_TICK + r, spans - 1))
-
-        @pl.when(kp == span_ticks)
+                wx(first, j).wait_recv()
+
+        for direction in (right, left):
+            a_item(direction, n)
+            h_item(direction, n)
+
+        @pl.when((first >= 0) & (first < CHUNKS))
+        def _():
+            hid_out[:, cols(first)] = partial(first, o)
+
+        @pl.when(k < spans)
+        def _():
+            project(k)
+
+        @pl.when(k == spans)
         def _():
             for j in range(1, TEN):
                 att(j).start()
 
-        cf = c0 - LAG
-
-        @pl.when((lax.rem(k, HOPS) == 0) & (cf >= 0))
-        def _():
-            @pl.when(o > 0)
-            def _():
-                h_r(cf, o).wait_recv()
-                hid_out[:, cols(cf)] += h_right[cf, o].astype(jnp.float32)
-
-            @pl.when(o < OUT - 1)
-            def _():
-                h_l(cf, o).wait_recv()
-                hid_out[:, cols(cf)] += h_left[cf, o].astype(jnp.float32)
-
-            hid_out[:, cols(cf)] *= gelu_slope(pre[:, cols(cf)].astype(jnp.float32))
-
-    loop((CHUNKS + LAG) * HOPS, tick)
+        m = n - 1 - DELAY - (OUT - 2) * GROUP
+        turn = (OUT - 1) * GROUP
+        rest = lax.rem(m, turn)
+
+        @pl.when((m >= 0) & (rest < GROUP) & (m // turn * GROUP < CHUNKS))
+        def _():
+            weight_chunk(m // turn * GROUP + rest)
+
+    loop(OUT * CHUNKS - GROUP, tick)
 
     total = part[pl.ds(pl.multiple_of(t * rows, rows), rows), :].astype(jnp.float32)
     total = total + bias[...].astype(jnp.float32)[None, :]
@@ -368,15 +338,6 @@
     att_out[...] = total
 
     factor = 1.0 / (OUT * INN)
-
-    def finish(c):
-        acc = wg_out[:, cols(c)]
-        for j in range(1, INN):
-            gx(c, j).wait_recv()
-            acc = acc + g_recv[c, j - 1].astype(jnp.float32)
-        wg_out[:, cols(c)] = acc * factor
-
-    loop(CHUNKS, finish)
 
     for j in range(1, OUT):
         uz(j).wait_send()
@@ -388,7 +349,26 @@
     for j in range(1, TEN):
         att(j).wait_send()
 
-    def drain(c):
+    def finish(c):
+        acc = wg_out[:, cols(c)]
+        for j in range(1, INN):
+            gx(c, j).wait_recv()
+            acc = acc + g_recv[c, j - 1].astype(jnp.float32)
+        wg_out[:, cols(c)] = acc * factor
+        slope = gelu_slope(pre[:, cols(c)].astype(jnp.float32))
+
+        @pl.when(o > 0)
+        def _():
+            h_r(c, o).wait_recv()
+            hid_out[:, cols(c)] += h_right[c, o].astype(jnp.float32)
+
+        @pl.when(o < OUT - 1)
+        def _():
+            h_l(c, o).wait_recv()
+            hid_out[:, cols(c)] += h_left[c, o].astype(jnp.float32)
+
+        hid_out[:, cols(c)] *= slope
+
         for j in range(1, INN):
             wx(c, j).wait_send()
             gx(c, j).wait_send()
@@ -405,13 +385,13 @@
 
             @pl.when((o < OUT - 1) & (o >= s))
             def _():
-                a_right(c, s, s == 0).wait_send()
+                a_right(c, s).wait_send()
 
             @pl.when((o > 0) & (o + s <= OUT - 1))
             def _():
-                a_left(c, s, s == 0).wait_send()
-
-    loop(CHUNKS, drain)
+                a_left(c, s).wait_send()
+
+    loop(CHUNKS, finish)
 
 
 def write_out(att, hid, wg, att_hbm, hid_hbm, wg_hbm, sem):
@@ -446,7 +426,7 @@
             pltpu.VMEM((tokens, ff), f32),
             pltpu.VMEM((rows_w, ff), f32),
         ),
-        in_specs=[anym, vmem, anym, vmem, anym, vmem, anym],
+        in_specs=[anym, vmem, anym, vmem, anym, anym, anym],
         out_specs=(vmem, vmem, vmem),
         scratch_shapes=[
             pltpu.VMEM(qkv.shape, bf),
@@ -458,13 +438,13 @@
             pltpu.VMEM((INN * rows_w, OUT * tokens), bf),
             pltpu.VMEM((CHUNKS, INN * rows_w, fc), bf),
             pltpu.VMEM((CHUNKS, OUT * tokens, fc), bf),
-            pltpu.VMEM((CHUNKS, tokens, fc), bf),
+            pltpu.VMEM((tokens, ff), bf),
             pltpu.VMEM((tokens // block, block, block), f32),
             pltpu.VMEM((CHUNKS, OUT, tokens, fc), bf),
             pltpu.VMEM((CHUNKS, OUT, tokens, fc), bf),
             pltpu.VMEM((CHUNKS, INN - 1, rows_w, fc), bf),
             pltpu.VMEM((CHUNKS, INN - 1, rows_w, fc), bf),
-            dma(3), dma(1, CHUNKS), dma(TEN - 1), dma(TEN - 1),
+            dma(4), dma(1, CHUNKS), dma(TEN - 1), dma(TEN - 1),
             dma(OUT - 1), dma(OUT - 1),
             dma(OUT, max(TEN // 2 - 1, 1)), dma(OUT, max(TEN // 2 - 1, 1)),
             dma(OUT, TEN // 2), dma(OUT, TEN // 2),

time: 135 us -> 117 us (0.87)
  the two profiles are of different devices: /device:TPU:1 before, /device:TPU:8 now
where the time goes in v2:
time: 117 us
  Pallas kernels  116 us (99%)
    pallas_call x1, Pallas kernels, body(): pl.pallas_call(functools.partial(kernel, sizes), out_shape=(pltpu.VMEM((r...  113 us
    pallas_call x1, Pallas kernels, body(): pl.pallas_call(write_out, out_shape=tuple((jax.ShapeDtypeStruct(r.shape,...  3.09 us

profile of v2, /device:TPU:8, one launch (start us, length us, event | category | flops | bytes accessed | tf_op | source)
XLA Modules:
  0.0 117.0 jit_solution(382731662295826066)
XLA Ops:
  0.6 113.3 %layer.1 = (f32[64,4096]{1,0:T(8,128)S(1)}, f32[256,2048]{1,0:T(8,128)S(1)}, f32[512,2048]{1,0:T(8,128)S(1)}) custom-call(bf16[3,256,1024]{2,1,0:T(8,128)(2,1)} %qkv_hbm.1, s32[1,4,64]{2,1,0:T(4,128)} %segments.1, bf16[4096,1024]{1,0:T(8,128)(2,1)} %ow_hbm.1, bf16[4096]{0:T(1024)(128)(2,1)} %bias.1, bf16[64,4096]{1,0:T(8,128)(2,1)} %up_hbm.1, ...), custom_call_target="tpu_custom_call" | custom-call | tf_op jit(solution)/shard_map/layer/pallas_call | solution.py:422
  113.9 3.1 %write_out.1 = (f32[64,4096]{1,0:T(8,128)}, f32[256,2048]{1,0:T(8,128)}, f32[512,2048]{1,0:T(8,128)}) custom-call(f32[64,4096]{1,0:T(8,128)S(1)} %get-tuple-element.6.att, f32[256,2048]{1,0:T(8,128)S(1)} %get-tuple-element.7.hid, f32[512,2048]{1,0:T(8,128)S(1)} %get-tuple-element.8.wg), custom_call_target="tpu_custom_call" | custom-call | tf_op jit(solution)/shard_map/write_out/pallas_call | solution.py:465

commit v3 on v2

--- a/solution.py
+++ b/solution.py
@@ -35,7 +35,7 @@
     qkv_hbm, segments, ow_hbm, bias, up_hbm, pre_hbm, w_hbm,
     att_out, hid_out, wg_out,
     qkv, ow, ctx, part, att_recv,
-    u_all, u_t, w_all, a_all, pre, same_ref, h_right, h_left, g_send, g_recv,
+    up, u_all, u_t, w_all, a_all, pre, same_ref, h_right, h_left, g_send, g_recv,
     local_sem, loc_wa, att_s, att_r,
     uz_s, uz_r, ux_s, ux_r, uc_s, uc_r,
     w_s, w_r, ar_s, ar_r, al_s, al_r,
@@ -76,7 +76,7 @@
     def uz(j):
         to = lax.rem(o + j, OUT)
         return remote(
-            up_hbm.at[:, pl.ds(pl.multiple_of(to * dcols, dcols), dcols)],
+            up.at[:, pl.ds(pl.multiple_of(to * dcols, dcols), dcols)],
             u_rows(o, t), uz_s.at[j - 1], uz_r.at[j - 1], to * INN + i, t,
         )
 
@@ -129,17 +129,26 @@
             return carry
         lax.fori_loop(0, count, step, 0)
 
-    own_u = pltpu.make_async_copy(
-        up_hbm.at[:, pl.ds(pl.multiple_of(o * dcols, dcols), dcols)], u_rows(o, t), local_sem.at[0])
+    load_up = pltpu.make_async_copy(up_hbm, up, local_sem.at[0])
     load_qkv = pltpu.make_async_copy(qkv_hbm, qkv, local_sem.at[1])
     load_ow = pltpu.make_async_copy(ow_hbm, ow, local_sem.at[2])
-
     load_pre = pltpu.make_async_copy(pre_hbm, pre, local_sem.at[3])
 
+    partners = (
+        [(lax.rem(o + j, OUT) * INN + i, t) for j in range(1, OUT)]
+        + [(o * INN + lax.rem(i + j, INN), t) for j in range(1, INN)]
+        + [(g, lax.rem(t + j, TEN)) for j in range(1, TEN)])
+    barrier = pltpu.get_barrier_semaphore()
+    for dp, tensor in partners:
+        pl.semaphore_signal(barrier, inc=1, device_id={"dp": dp, "tensor": tensor},
+                            device_id_type=pl.DeviceIdType.MESH)
+
+    load_up.start()
+    load_pre.start()
+    load_up.wait()
+    pl.semaphore_wait(barrier, len(partners))
     for j in range(1, OUT):
         uz(j).start()
-    load_pre.start()
-    own_u.start()
 
     def start_w(c):
         for j in range(1, INN):
@@ -149,6 +158,8 @@
     loop(CHUNKS, start_w)
     load_qkv.start()
     load_ow.start()
+    u_all[pl.ds(pl.multiple_of((o * TEN + t) * rows, rows), rows), :] = (
+        up[:, pl.ds(pl.multiple_of(o * dcols, dcols), dcols)])
 
     right = (o, lambda p: p, a_right, ar_r, h_right, h_r)
     left = (OUT - 1 - o, lambda p: OUT - 1 - p, a_left, al_r, h_left, h_l)
@@ -183,7 +194,6 @@
 
     load_pre.wait()
     loop(GROUP, open_group)
-    own_u.wait()
     for k in range(1, XS):
         ux(0, k).start()
     uc(0, 0).start()
@@ -434,6 +444,7 @@
             pltpu.VMEM((tokens, qkv.shape[2]), bf),
             pltpu.VMEM((tokens, width), bf),
             pltpu.VMEM((TEN - 1, rows, width), bf),
+            pltpu.VMEM((rows, width), bf),
             pltpu.VMEM((OUT * tokens, INN * rows_w), bf),
             pltpu.VMEM((INN * rows_w, OUT * tokens), bf),
             pltpu.VMEM((CHUNKS, INN * rows_w, fc), bf),
@@ -456,7 +467,7 @@
             dma(CHUNKS, INN - 1), dma(CHUNKS, INN - 1),
         ],
         compiler_params=pltpu.CompilerParams(
-            has_side_effects=True, vmem_limit_bytes=64_000_000 - held),
+            has_side_effects=True, collective_id=0, vmem_limit_bytes=64_000_000 - held),
         name="layer",
     )(qkv, segment_ids, out_weight, out_bias, upstream, pre_act, down_weight)
     results = tuple(

time: 117 us -> 113 us (0.966)
  Pallas kernels: 116 us -> 112 us
    pallas_call x1, Pallas kernels: 113 us -> 109 us  [body(): pl.pallas_call(functools.partial(kernel, sizes), out_shape=(pltpu.VMEM((r...]
where the time goes in v3:
time: 113 us; the launch traced here: 112 us
  Pallas kernels  112 us (99%)
    pallas_call x1, Pallas kernels, body(): pl.pallas_call(functools.partial(kernel, sizes), out_shape=(pltpu.VMEM((r...  109 us
    pallas_call x1, Pallas kernels, body(): pl.pallas_call(write_out, out_shape=tuple((jax.ShapeDtypeStruct(r.shape,...  3.09 us

profile of v3, /device:TPU:8, one launch (start us, length us, event | category | flops | bytes accessed | tf_op | source)
XLA Modules:
  0.0 112.5 jit_solution(17937058323798541280)
XLA Ops:
  0.6 108.7 %layer.1 = (f32[64,4096]{1,0:T(8,128)S(1)}, f32[256,2048]{1,0:T(8,128)S(1)}, f32[512,2048]{1,0:T(8,128)S(1)}) custom-call(bf16[3,256,1024]{2,1,0:T(8,128)(2,1)} %qkv_hbm.1, s32[1,4,64]{2,1,0:T(4,128)} %segments.1, bf16[4096,1024]{1,0:T(8,128)(2,1)} %ow_hbm.1, bf16[4096]{0:T(1024)(128)(2,1)} %bias.1, bf16[64,4096]{1,0:T(8,128)(2,1)} %up_hbm.1, ...), custom_call_target="tpu_custom_call" | custom-call | tf_op jit(solution)/shard_map/layer/pallas_call | solution.py:432
  109.4 3.1 %write_out.1 = (f32[64,4096]{1,0:T(8,128)}, f32[256,2048]{1,0:T(8,128)}, f32[512,2048]{1,0:T(8,128)}) custom-call(f32[64,4096]{1,0:T(8,128)S(1)} %get-tuple-element.6.att, f32[256,2048]{1,0:T(8,128)S(1)} %get-tuple-element.7.hid, f32[512,2048]{1,0:T(8,128)S(1)} %get-tuple-element.8.wg), custom_call_target="tpu_custom_call" | custom-call | tf_op jit(solution)/shard_map/write_out/pallas_call | solution.py:476

commit v4 on v3

--- a/solution.py
+++ b/solution.py
@@ -32,14 +32,14 @@
 
 def kernel(
     sizes,
-    qkv_hbm, segments, ow_hbm, bias, up_hbm, pre_hbm, w_hbm,
+    qkv_hbm, names_hbm, ow_hbm, bias_hbm, up_hbm, pre_hbm, w_hbm,
     att_out, hid_out, wg_out,
-    qkv, ow, ctx, part, att_recv,
+    segments, bias, qkv, ow, ctx, part, att_recv,
     up, u_all, u_t, w_all, a_all, pre, same_ref, h_right, h_left, g_send, g_recv,
     local_sem, loc_wa, att_s, att_r,
     uz_s, uz_r, ux_s, ux_r, uc_s, uc_r,
     w_s, w_r, ar_s, ar_r, al_s, al_r,
-    hr_s, hr_r, hl_s, hl_r, g_s, g_r,
+    hr_s, hr_r, hl_s, hl_r, g_s, g_r, far_sem,
 ):
     OUT, INN, TEN = sizes
     XS = TEN // 2
@@ -134,28 +134,73 @@
     load_ow = pltpu.make_async_copy(ow_hbm, ow, local_sem.at[2])
     load_pre = pltpu.make_async_copy(pre_hbm, pre, local_sem.at[3])
 
+    load_names = pltpu.make_async_copy(names_hbm, segments, local_sem.at[4])
+    load_bias = pltpu.make_async_copy(bias_hbm, bias, local_sem.at[5])
+
+    def signal(semaphore, dp, tensor):
+        pl.semaphore_signal(semaphore, inc=1, device_id={"dp": dp, "tensor": tensor},
+                            device_id_type=pl.DeviceIdType.MESH)
+
+    load_up.start()
+    load_pre.start()
     partners = (
-        [(lax.rem(o + j, OUT) * INN + i, t) for j in range(1, OUT)]
-        + [(o * INN + lax.rem(i + j, INN), t) for j in range(1, INN)]
+        [(o * INN + lax.rem(i + j, INN), t) for j in range(1, INN)]
         + [(g, lax.rem(t + j, TEN)) for j in range(1, TEN)])
     barrier = pltpu.get_barrier_semaphore()
+
+    @pl.when(o < OUT - 1)
+    def _():
+        signal(barrier, jnp.minimum(o + 1, OUT - 1) * INN + i, t)
+
+    @pl.when(o > 0)
+    def _():
+        signal(barrier, jnp.maximum(o - 1, 0) * INN + i, t)
+
     for dp, tensor in partners:
-        pl.semaphore_signal(barrier, inc=1, device_id={"dp": dp, "tensor": tensor},
-                            device_id_type=pl.DeviceIdType.MESH)
-
-    load_up.start()
-    load_pre.start()
+        signal(barrier, dp, tensor)
     load_up.wait()
-    pl.semaphore_wait(barrier, len(partners))
+    sides = jnp.minimum(o, 1) + jnp.minimum(OUT - 1 - o, 1)
+    pl.semaphore_wait(barrier, len(partners) + sides)
+
+    def uz_near(to):
+        return (to - o == 1) | (o - to == 1)
+
     for j in range(1, OUT):
-        uz(j).start()
+        @pl.when(uz_near(lax.rem(o + j, OUT)))
+        def _():
+            uz(j).start()
 
     def start_w(c):
         for j in range(1, INN):
             wx(c, j).start()
         own_w(c).start()
 
-    loop(CHUNKS, start_w)
+    if OUT > 2:
+        @pl.when(o >= 2)
+        def _():
+            pl.semaphore_wait(far_sem.at[0], 1)
+
+        @pl.when((o >= 1) & (o <= OUT - 2))
+        def _():
+            signal(far_sem.at[0], jnp.minimum(o + 1, OUT - 1) * INN + i, t)
+
+        loop(CHUNKS, start_w)
+
+        @pl.when(o <= OUT - 3)
+        def _():
+            pl.semaphore_wait(far_sem.at[1], 1)
+
+        @pl.when((o >= 1) & (o <= OUT - 2))
+        def _():
+            signal(far_sem.at[1], jnp.maximum(o - 1, 0) * INN + i, t)
+    else:
+        loop(CHUNKS, start_w)
+    for j in range(1, OUT):
+        @pl.when(jnp.logical_not(uz_near(lax.rem(o + j, OUT))))
+        def _():
+            uz(j).start()
+    load_names.start()
+    load_bias.start()
     load_qkv.start()
     load_ow.start()
     u_all[pl.ds(pl.multiple_of((o * TEN + t) * rows, rows), rows), :] = (
@@ -203,6 +248,8 @@
     block = min(tokens, 4 * ROWS_DEV)
     scale = 1.0 / math.sqrt(HEAD)
 
+    load_names.wait()
+    load_bias.wait()
     labels = segments[0].astype(jnp.float32)
     packs, length = labels.shape
     spread = (
@@ -365,24 +412,44 @@
             gx(c, j).wait_recv()
             acc = acc + g_recv[c, j - 1].astype(jnp.float32)
         wg_out[:, cols(c)] = acc * factor
-        slope = gelu_slope(pre[:, cols(c)].astype(jnp.float32))
-
-        @pl.when(o > 0)
-        def _():
-            h_r(c, o).wait_recv()
-            hid_out[:, cols(c)] += h_right[c, o].astype(jnp.float32)
-
-        @pl.when(o < OUT - 1)
-        def _():
-            h_l(c, o).wait_recv()
-            hid_out[:, cols(c)] += h_left[c, o].astype(jnp.float32)
-
-        hid_out[:, cols(c)] *= slope
-
         for j in range(1, INN):
             wx(c, j).wait_send()
             gx(c, j).wait_send()
         for s in range(OUT - 1):
+            @pl.when((o < OUT - 1) & (o >= s))
+            def _():
+                a_right(c, s).wait_send()
+
+            @pl.when((o > 0) & (o + s <= OUT - 1))
+            def _():
+                a_left(c, s).wait_send()
+
+    loop(CHUNKS, finish)
+
+    def close(c):
+        slope = gelu_slope(pre[:, cols(c)].astype(jnp.float32))
+
+        @pl.when(o == 0)
+        def _():
+            h_l(c, o).wait_recv()
+            hid_out[:, cols(c)] = (
+                hid_out[:, cols(c)] + h_left[c, o].astype(jnp.float32)) * slope
+
+        @pl.when(o == OUT - 1)
+        def _():
+            h_r(c, o).wait_recv()
+            hid_out[:, cols(c)] = (
+                hid_out[:, cols(c)] + h_right[c, o].astype(jnp.float32)) * slope
+
+        @pl.when((o > 0) & (o < OUT - 1))
+        def _():
+            h_r(c, o).wait_recv()
+            h_l(c, o).wait_recv()
+            hid_out[:, cols(c)] = (
+                hid_out[:, cols(c)] + h_right[c, o].astype(jnp.float32)
+                + h_left[c, o].astype(jnp.float32)) * slope
+
+        for s in range(OUT - 1):
             er, el = OUT - 1 - s, s
 
             @pl.when(o < er)
@@ -393,15 +460,7 @@
             def _():
                 h_l(c, el).wait_send()
 
-            @pl.when((o < OUT - 1) & (o >= s))
-            def _():
-                a_right(c, s).wait_send()
-
-            @pl.when((o > 0) & (o + s <= OUT - 1))
-            def _():
-                a_left(c, s).wait_send()
-
-    loop(CHUNKS, finish)
+    loop(CHUNKS, close)
 
 
 def write_out(att, hid, wg, att_hbm, hid_hbm, wg_hbm, sem):
@@ -436,9 +495,11 @@
             pltpu.VMEM((tokens, ff), f32),
             pltpu.VMEM((rows_w, ff), f32),
         ),
-        in_specs=[anym, vmem, anym, vmem, anym, anym, anym],
+        in_specs=[anym] * 7,
         out_specs=(vmem, vmem, vmem),
         scratch_shapes=[
+            pltpu.VMEM(segment_ids.shape, segment_ids.dtype),
+            pltpu.VMEM(out_bias.shape, bf),
             pltpu.VMEM(qkv.shape, bf),
             pltpu.VMEM(out_weight.shape, bf),
             pltpu.VMEM((tokens, qkv.shape[2]), bf),
@@ -455,7 +516,7 @@
             pltpu.VMEM((CHUNKS, OUT, tokens, fc), bf),
             pltpu.VMEM((CHUNKS, INN - 1, rows_w, fc), bf),
             pltpu.VMEM((CHUNKS, INN - 1, rows_w, fc), bf),
-            dma(4), dma(1, CHUNKS), dma(TEN - 1), dma(TEN - 1),
+            dma(6), dma(1, CHUNKS), dma(TEN - 1), dma(TEN - 1),
             dma(OUT - 1), dma(OUT - 1),
             dma(OUT, max(TEN // 2 - 1, 1)), dma(OUT, max(TEN // 2 - 1, 1)),
             dma(OUT, TEN // 2), dma(OUT, TEN // 2),
@@ -465,6 +526,7 @@
             dma(CHUNKS, OUT), dma(CHUNKS, OUT),
             dma(CHUNKS, OUT), dma(CHUNKS, OUT),
             dma(CHUNKS, INN - 1), dma(CHUNKS, INN - 1),
+            pltpu.SemaphoreType.REGULAR((2,)),
         ],
         compiler_params=pltpu.CompilerParams(
             has_side_effects=True, collective_id=0, vmem_limit_bytes=64_000_000 - held),

time: 113 us -> 112 us (level)
  no operation moved by 1% of the time
where the time goes in v4:
time: 112 us
  Pallas kernels  111 us (99%)
    pallas_call x1, Pallas kernels, body(): pl.pallas_call(functools.partial(kernel, sizes), out_shape=(pltpu.VMEM((r...  108 us
    pallas_call x1, Pallas kernels, body(): pl.pallas_call(write_out, out_shape=tuple((jax.ShapeDtypeStruct(r.shape,...  3.09 us

profile of v4, /device:TPU:8, one launch (start us, length us, event | category | flops | bytes accessed | tf_op | source)
XLA Modules:
  0.0 111.8 jit_solution(15159103372993093377)
XLA Ops:
  0.6 108.0 %layer.1 = (f32[64,4096]{1,0:T(8,128)S(1)}, f32[256,2048]{1,0:T(8,128)S(1)}, f32[512,2048]{1,0:T(8,128)S(1)}) custom-call(bf16[3,256,1024]{2,1,0:T(8,128)(2,1)} %qkv_hbm.1, s32[1,4,64]{2,1,0:T(4,128)} %names_hbm.1, bf16[4096,1024]{1,0:T(8,128)(2,1)} %ow_hbm.1, bf16[4096]{0:T(1024)(128)(2,1)} %bias_hbm.1, bf16[64,4096]{1,0:T(8,128)(2,1)} %up_hbm.1, ...), custom_call_target="tpu_custom_call" | custom-call | tf_op jit(solution)/shard_map/layer/pallas_call | solution.py:491
  108.7 3.1 %write_out.1 = (f32[64,4096]{1,0:T(8,128)}, f32[256,2048]{1,0:T(8,128)}, f32[512,2048]{1,0:T(8,128)}) custom-call(f32[64,4096]{1,0:T(8,128)S(1)} %get-tuple-element.6.att, f32[256,2048]{1,0:T(8,128)S(1)} %get-tuple-element.7.hid, f32[512,2048]{1,0:T(8,128)S(1)} %get-tuple-element.8.wg), custom_call_target="tpu_custom_call" | custom-call | tf_op jit(solution)/shard_map/write_out/pallas_call | solution.py:538

commit v5 on v4

--- a/solution.py
+++ b/solution.py
@@ -10,9 +10,9 @@
 
 HEAD = 128
 ROWS_DEV = 64
-CHUNKS = 8
-GROUP = 4
-DELAY = 2
+CHUNKS = 4
+GROUP = 2
+DELAY = 1
 PIECES = 4
 
 root_half = 1.0 / math.sqrt(2.0)

time: 112 us -> 111 us (level)
  no operation moved by 1% of the time
where the time goes in v5:
time: 111 us
  Pallas kernels  110 us (99%)
    pallas_call x1, Pallas kernels, body(): pl.pallas_call(functools.partial(kernel, sizes), out_shape=(pltpu.VMEM((r...  107 us
    pallas_call x1, Pallas kernels, body(): pl.pallas_call(write_out, out_shape=tuple((jax.ShapeDtypeStruct(r.shape,...  3.09 us

profile of v5, /device:TPU:8, one launch (start us, length us, event | category | flops | bytes accessed | tf_op | source)
XLA Modules:
  0.0 110.6 jit_solution(8872461602975545718)
XLA Ops:
  0.6 106.9 %layer.1 = (f32[64,4096]{1,0:T(8,128)S(1)}, f32[256,2048]{1,0:T(8,128)S(1)}, f32[512,2048]{1,0:T(8,128)S(1)}) custom-call(bf16[3,256,1024]{2,1,0:T(8,128)(2,1)} %qkv_hbm.1, s32[1,4,64]{2,1,0:T(4,128)} %names_hbm.1, bf16[4096,1024]{1,0:T(8,128)(2,1)} %ow_hbm.1, bf16[4096]{0:T(1024)(128)(2,1)} %bias_hbm.1, bf16[64,4096]{1,0:T(8,128)(2,1)} %up_hbm.1, ...), custom_call_target="tpu_custom_call" | custom-call | tf_op jit(solution)/shard_map/layer/pallas_call | solution.py:491
  107.6 3.1 %write_out.1 = (f32[64,4096]{1,0:T(8,128)}, f32[256,2048]{1,0:T(8,128)}, f32[512,2048]{1,0:T(8,128)}) custom-call(f32[64,4096]{1,0:T(8,128)S(1)} %get-tuple-element.6.att, f32[256,2048]{1,0:T(8,128)S(1)} %get-tuple-element.7.hid, f32[512,2048]{1,0:T(8,128)S(1)} %get-tuple-element.8.wg), custom_call_target="tpu_custom_call" | custom-call | tf_op jit(solution)/shard_map/write_out/pallas_call | solution.py:538

commit v6 on v5

--- a/solution.py
+++ b/solution.py
@@ -36,10 +36,7 @@
     att_out, hid_out, wg_out,
     segments, bias, qkv, ow, ctx, part, att_recv,
     up, u_all, u_t, w_all, a_all, pre, same_ref, h_right, h_left, g_send, g_recv,
-    local_sem, loc_wa, att_s, att_r,
-    uz_s, uz_r, ux_s, ux_r, uc_s, uc_r,
-    w_s, w_r, ar_s, ar_r, al_s, al_r,
-    hr_s, hr_r, hl_s, hl_r, g_s, g_r, far_sem,
+    local_sem, send_sem, z_r, uz_r, w_r, all_r, far_sem,
 ):
     OUT, INN, TEN = sizes
     XS = TEN // 2
@@ -77,51 +74,57 @@
         to = lax.rem(o + j, OUT)
         return remote(
             up.at[:, pl.ds(pl.multiple_of(to * dcols, dcols), dcols)],
-            u_rows(o, t), uz_s.at[j - 1], uz_r.at[j - 1], to * INN + i, t,
+            u_rows(o, t), send_sem.at[2], uz_r.at[j - 1], to * INN + i, t,
         )
 
     def ux(j, k):
         block = u_rows(lax.rem(o - j + OUT, OUT), t)
-        return remote(block, block, ux_s.at[j, k - 1], ux_r.at[j, k - 1], g,
+        return remote(block, block, send_sem.at[3], all_r.at[0], g,
                       lax.rem(x + k, XS) * 2 + core)
 
     def uc(j, k):
         block = u_rows(lax.rem(o - j + OUT, OUT), lax.rem(x - k + XS, XS) * 2 + core)
-        return remote(block, block, uc_s.at[j, k], uc_r.at[j, k], g, x * 2 + 1 - core)
+        return remote(block, block, send_sem.at[4], all_r.at[1], g, x * 2 + 1 - core)
 
     def wx(c, j):
-        return remote(w_hbm.at[:, cols(c)], w_rows(c, i), w_s.at[c, j - 1], w_r.at[c, j - 1],
+        return remote(w_hbm.at[:, cols(c)], w_rows(c, i), send_sem.at[5], w_r.at[c],
                       o * INN + lax.rem(i + j, INN), t)
 
-    def a_right(c, s):
+    def a_right(c, s, n):
         block = a_rows(c, jnp.maximum(o - s, 0))
-        return remote(block, block, ar_s.at[c, s], ar_r.at[c, s],
+        return remote(block, block, send_sem.at[0], z_r.at[0, n],
                       jnp.minimum(o + 1, OUT - 1) * INN + i, t)
 
-    def a_left(c, s):
+    def a_left(c, s, n):
         block = a_rows(c, jnp.minimum(o + s, OUT - 1))
-        return remote(block, block, al_s.at[c, s], al_r.at[c, s],
+        return remote(block, block, send_sem.at[1], z_r.at[1, n],
                       jnp.maximum(o - 1, 0) * INN + i, t)
 
-    def h_r(c, e):
-        return remote(h_right.at[c, e], h_right.at[c, e], hr_s.at[c, e], hr_r.at[c, e],
+    def h_r(c, e, n):
+        return remote(h_right.at[c, e], h_right.at[c, e], send_sem.at[0], z_r.at[0, n],
                       jnp.minimum(o + 1, OUT - 1) * INN + i, t)
 
-    def h_l(c, e):
-        return remote(h_left.at[c, e], h_left.at[c, e], hl_s.at[c, e], hl_r.at[c, e],
+    def h_l(c, e, n):
+        return remote(h_left.at[c, e], h_left.at[c, e], send_sem.at[1], z_r.at[1, n],
                       jnp.maximum(o - 1, 0) * INN + i, t)
 
     def gx(c, j):
-        return remote(g_send.at[c, j - 1], g_recv.at[c, j - 1], g_s.at[c, j - 1], g_r.at[c, j - 1],
+        return remote(g_send.at[c, j - 1], g_recv.at[c, j - 1], send_sem.at[6], all_r.at[3],
                       o * INN + lax.rem(i + j, INN), t)
 
     def att(j):
         to = lax.rem(t + j, TEN)
         return remote(part.at[pl.ds(pl.multiple_of(to * rows, rows), rows), :],
-                      att_recv.at[j - 1], att_s.at[j - 1], att_r.at[j - 1], g, to)
+                      att_recv.at[j - 1], send_sem.at[7], all_r.at[2], g, to)
 
     def own_w(c):
-        return pltpu.make_async_copy(w_hbm.at[:, cols(c)], w_rows(c, i), loc_wa.at[0, c])
+        return pltpu.make_async_copy(w_hbm.at[:, cols(c)], w_rows(c, i), local_sem.at[6])
+
+    def sent(ref, stream):
+        remote(ref, ref, send_sem.at[stream], send_sem.at[stream], g, t).wait_send()
+
+    def landed(ref, semaphore):
+        remote(ref, ref, semaphore, semaphore, g, t).wait_recv()
 
     def loop(count, fn):
         def step(index, carry):
@@ -130,6 +133,8 @@
         lax.fori_loop(0, count, step, 0)
 
     load_up = pltpu.make_async_copy(up_hbm, up, local_sem.at[0])
+    near = sorted({1, OUT - 1})
+    far = list(range(2, OUT - 1))
     load_qkv = pltpu.make_async_copy(qkv_hbm, qkv, local_sem.at[1])
     load_ow = pltpu.make_async_copy(ow_hbm, ow, local_sem.at[2])
     load_pre = pltpu.make_async_copy(pre_hbm, pre, local_sem.at[3])
@@ -165,11 +170,10 @@
     def uz_near(to):
         return (to - o == 1) | (o - to == 1)
 
-    for j in range(1, OUT):
+    for j in near:
         @pl.when(uz_near(lax.rem(o + j, OUT)))
         def _():
             uz(j).start()
-
     def start_w(c):
         for j in range(1, INN):
             wx(c, j).start()
@@ -206,13 +210,13 @@
     u_all[pl.ds(pl.multiple_of((o * TEN + t) * rows, rows), rows), :] = (
         up[:, pl.ds(pl.multiple_of(o * dcols, dcols), dcols)])
 
-    right = (o, lambda p: p, a_right, ar_r, h_right, h_r)
-    left = (OUT - 1 - o, lambda p: OUT - 1 - p, a_left, al_r, h_left, h_l)
+    right = (o, lambda p: p, a_right, z_r.at[0], h_right, h_r)
+    left = (OUT - 1 - o, lambda p: OUT - 1 - p, a_left, z_r.at[1], h_left, h_l)
 
     def a_wait(direction, c, s):
         r, place, _, arrived, _, _ = direction
-        got = a_rows(c, place(jnp.maximum(r - s, 0)))
-        remote(got, got, arrived.at[c, s - 1], arrived.at[c, s - 1], g, t).wait_recv()
+        step = c // GROUP * GROUP * r + (s - 1) * GROUP + lax.rem(c, GROUP)
+        landed(a_rows(c, place(jnp.maximum(r - s, 0))), arrived.at[step])
 
     def a_item(direction, n):
         r, _, copy, _, _, _ = direction
@@ -226,7 +230,7 @@
             @pl.when(s > 0)
             def _():
                 a_wait(direction, c, s)
-            copy(c, s).start()
+            copy(c, s, n).start()
 
     def activate(c):
         act = gelu_exact(pre[:, cols(c)].astype(jnp.float32)).astype(jnp.bfloat16)
@@ -299,7 +303,7 @@
         return jnp.dot(u_all[span, :], w_all[c], preferred_element_type=jnp.float32)
 
     def h_item(direction, n):
-        r, place, _, _, held, copy = direction
+        r, place, _, arrived, held, copy = direction
         m = n - (r + 1) * CHUNKS
         e = place(OUT - 1 - m // CHUNKS)
         c = lax.rem(m, CHUNKS)
@@ -307,14 +311,14 @@
         @pl.when((m >= 0) & (r == 0))
         def _():
             held[c, e] = partial(c, e).astype(jnp.bfloat16)
-            copy(c, e).start()
+            copy(c, e, n).start()
 
         @pl.when((m >= 0) & (r > 0) & (r < OUT - 1))
         def _():
             mine = partial(c, e)
-            copy(c, e).wait_recv()
+            landed(held.at[c, e], arrived.at[n - CHUNKS])
             held[c, e] = (mine + held[c, e].astype(jnp.float32)).astype(jnp.bfloat16)
-            copy(c, e).start()
+            copy(c, e, n).start()
 
     def weight_chunk(c):
         for direction in (right, left):
@@ -340,44 +344,53 @@
         for k in range(1, XS):
             ux(j, k).start()
         uc(j, 0).start()
+    load_ow.wait()
+    early = spans // 2
+    loop(early, project)
+
+    def relay(n):
+        a_item(right, n)
+        a_item(left, n)
+
+    loop(CHUNKS - GROUP - 1, lambda n: relay(n + GROUP))
+    if XS > 1:
+        landed(u_all.at[pl.ds(0, OUT * (XS - 1) * rows), :], all_r.at[0])
     for j in range(OUT):
         for k in range(1, XS):
-            ux(j, k).wait_recv()
             uc(j, k).start()
-    for j in range(OUT):
-        for k in range(XS):
-            uc(j, k).wait_recv()
+    relay(CHUNKS - 1)
+    landed(u_all.at[pl.ds(0, OUT * XS * rows), :], all_r.at[1])
     loop(OUT, flip)
-    load_ow.wait()
+    own_rows = g_send.at[:, 0]
+    pltpu.make_async_copy(own_rows, own_rows, local_sem.at[6]).wait()
+    lead = max(DELAY, CHUNKS - 1 - (OUT - 2) * GROUP) + 1 + (OUT - 2) * GROUP
 
     def tick(k):
-        n = k + GROUP
-        first = n - CHUNKS
-
-        @pl.when((first >= 0) & (first < CHUNKS))
-        def _():
-            own_w(first).wait()
-            for j in range(1, INN):
-                wx(first, j).wait_recv()
+        n = k + CHUNKS
+        first = k
+
+        @pl.when(first < CHUNKS)
+        def _():
+            landed(g_recv.at[first], w_r.at[first])
 
         for direction in (right, left):
             a_item(direction, n)
             h_item(direction, n)
 
-        @pl.when((first >= 0) & (first < CHUNKS))
+        @pl.when(first < CHUNKS)
         def _():
             hid_out[:, cols(first)] = partial(first, o)
 
-        @pl.when(k < spans)
-        def _():
-            project(k)
-
-        @pl.when(k == spans)
+        @pl.when(k < spans - early)
+        def _():
+            project(k + early)
+
+        @pl.when(k == spans - early)
         def _():
             for j in range(1, TEN):
                 att(j).start()
 
-        m = n - 1 - DELAY - (OUT - 2) * GROUP
+        m = n - lead
         turn = (OUT - 1) * GROUP
         rest = lax.rem(m, turn)
 
@@ -385,95 +398,78 @@
         def _():
             weight_chunk(m // turn * GROUP + rest)
 
-    loop(OUT * CHUNKS - GROUP, tick)
+    loop((OUT - 1) * CHUNKS, tick)
 
     total = part[pl.ds(pl.multiple_of(t * rows, rows), rows), :].astype(jnp.float32)
     total = total + bias[...].astype(jnp.float32)[None, :]
+    landed(att_recv, all_r.at[2])
     for j in range(1, TEN):
-        att(j).wait_recv()
         total = total + att_recv[j - 1].astype(jnp.float32)
     att_out[...] = total
 
     factor = 1.0 / (OUT * INN)
 
-    for j in range(1, OUT):
-        uz(j).wait_send()
-    for j in range(OUT):
-        for k in range(1, XS):
-            ux(j, k).wait_send()
-        for k in range(XS):
-            uc(j, k).wait_send()
-    for j in range(1, TEN):
-        att(j).wait_send()
+    landed(g_recv, all_r.at[3])
 
     def finish(c):
         acc = wg_out[:, cols(c)]
         for j in range(1, INN):
-            gx(c, j).wait_recv()
             acc = acc + g_recv[c, j - 1].astype(jnp.float32)
         wg_out[:, cols(c)] = acc * factor
-        for j in range(1, INN):
-            wx(c, j).wait_send()
-            gx(c, j).wait_send()
-        for s in range(OUT - 1):
-            @pl.when((o < OUT - 1) & (o >= s))
-            def _():
-                a_right(c, s).wait_send()
-
-            @pl.when((o > 0) & (o + s <= OUT - 1))
-            def _():
-                a_left(c, s).wait_send()
 
     loop(CHUNKS, finish)
+    sent(up.at[:, pl.ds(0, (OUT - 1) * dcols)], 2)
+    if XS > 1:
+        sent(u_all.at[pl.ds(0, OUT * (XS - 1) * rows), :], 3)
+    sent(u_all.at[pl.ds(0, OUT * XS * rows), :], 4)
+    sent(g_send, 5)
+    sent(g_send, 6)
+    sent(att_recv, 7)
+    final = (OUT - 1) * CHUNKS
 
     def close(c):
         slope = gelu_slope(pre[:, cols(c)].astype(jnp.float32))
 
         @pl.when(o == 0)
         def _():
-            h_l(c, o).wait_recv()
+            landed(h_left.at[c, o], z_r.at[1, final + c])
             hid_out[:, cols(c)] = (
                 hid_out[:, cols(c)] + h_left[c, o].astype(jnp.float32)) * slope
 
         @pl.when(o == OUT - 1)
         def _():
-            h_r(c, o).wait_recv()
+            landed(h_right.at[c, o], z_r.at[0, final + c])
             hid_out[:, cols(c)] = (
                 hid_out[:, cols(c)] + h_right[c, o].astype(jnp.float32)) * slope
 
         @pl.when((o > 0) & (o < OUT - 1))
         def _():
-            h_r(c, o).wait_recv()
-            h_l(c, o).wait_recv()
+            landed(h_right.at[c, o], z_r.at[0, final + c])
+            landed(h_left.at[c, o], z_r.at[1, final + c])
             hid_out[:, cols(c)] = (
                 hid_out[:, cols(c)] + h_right[c, o].astype(jnp.float32)
                 + h_left[c, o].astype(jnp.float32)) * slope
 
-        for s in range(OUT - 1):
-            er, el = OUT - 1 - s, s
-
-            @pl.when(o < er)
-            def _():
-                h_r(c, er).wait_send()
-
-            @pl.when(o > el)
-            def _():
-                h_l(c, el).wait_send()
-
     loop(CHUNKS, close)
 
+    @pl.when(o < OUT - 1)
+    def _():
+        sent(a_all, 0)
+
+    @pl.when(o > 0)
+    def _():
+        sent(a_all, 1)
+
 
 def write_out(att, hid, wg, att_hbm, hid_hbm, wg_hbm, sem):
-    copies = []
-    for n, (src, dst) in enumerate(((att, att_hbm), (hid, hid_hbm), (wg, wg_hbm))):
+    pairs = ((att, att_hbm), (hid, hid_hbm), (wg, wg_hbm))
+    for n, (src, dst) in enumerate(pairs):
         step = src.shape[0] // PIECES
         for p in range(PIECES):
             span = pl.ds(p * step, step)
-            copies.append(pltpu.make_async_copy(src.at[span, :], dst.at[span, :], sem.at[n, p]))
-    for copy in copies:
-        copy.start()
-    for copy in copies:
-        copy.wait()
+            pltpu.make_async_copy(src.at[span, :], dst.at[span, :], sem.at[n]).start()
+    for n, (src, dst) in enumerate(pairs):
+        pltpu.make_async_copy(src, dst, sem.at[n]).wait()
 
 
 def body(sizes, qkv, segment_ids, out_weight, out_bias, upstream, pre_act, down_weight):
@@ -516,16 +512,7 @@
             pltpu.VMEM((CHUNKS, OUT, tokens, fc), bf),
             pltpu.VMEM((CHUNKS, INN - 1, rows_w, fc), bf),
             pltpu.VMEM((CHUNKS, INN - 1, rows_w, fc), bf),
-            dma(6), dma(1, CHUNKS), dma(TEN - 1), dma(TEN - 1),
-            dma(OUT - 1), dma(OUT - 1),
-            dma(OUT, max(TEN // 2 - 1, 1)), dma(OUT, max(TEN // 2 - 1, 1)),
-            dma(OUT, TEN // 2), dma(OUT, TEN // 2),
-            dma(CHUNKS, INN - 1), dma(CHUNKS, INN - 1),
-            dma(CHUNKS, OUT - 1), dma(CHUNKS, OUT - 1),
-            dma(CHUNKS, OUT - 1), dma(CHUNKS, OUT - 1),
-            dma(CHUNKS, OUT), dma(CHUNKS, OUT),
-            dma(CHUNKS, OUT), dma(CHUNKS, OUT),
-            dma(CHUNKS, INN - 1), dma(CHUNKS, INN - 1),
+            dma(7), dma(8), dma(2, OUT * CHUNKS), dma(OUT - 1), dma(CHUNKS), dma(4),
             pltpu.SemaphoreType.REGULAR((2,)),
         ],
         compiler_params=pltpu.CompilerParams(
@@ -540,7 +527,7 @@
         out_shape=tuple(jax.ShapeDtypeStruct(r.shape, f32) for r in results),
         in_specs=[vmem] * 3,
         out_specs=(anym,) * 3,
-        scratch_shapes=[dma(3, PIECES)],
+        scratch_shapes=[dma(3)],
         compiler_params=pltpu.CompilerParams(vmem_limit_bytes=2**20),
         name="write_out",
     )(*results)

time: 111 us -> 110 us (level)
  no operation moved by 1% of the time
where the time goes in v6:
time: 110 us
  Pallas kernels  109 us (99%)
    pallas_call x1, Pallas kernels, body(): pl.pallas_call(functools.partial(kernel, sizes), out_shape=(pltpu.VMEM((r...  106 us
    pallas_call x1, Pallas kernels, body(): pl.pallas_call(write_out, out_shape=tuple((jax.ShapeDtypeStruct(r.shape,...  3.01 us

profile of v6, /device:TPU:8, one launch (start us, length us, event | category | flops | bytes accessed | tf_op | source)
XLA Modules:
  0.0 109.5 jit_solution(8096778702501400901)
XLA Ops:
  0.6 105.9 %layer.1 = (f32[64,4096]{1,0:T(8,128)S(1)}, f32[256,2048]{1,0:T(8,128)S(1)}, f32[512,2048]{1,0:T(8,128)S(1)}) custom-call(bf16[3,256,1024]{2,1,0:T(8,128)(2,1)} %qkv_hbm.1, s32[1,4,64]{2,1,0:T(4,128)} %names_hbm.1, bf16[4096,1024]{1,0:T(8,128)(2,1)} %ow_hbm.1, bf16[4096]{0:T(1024)(128)(2,1)} %bias_hbm.1, bf16[64,4096]{1,0:T(8,128)(2,1)} %up_hbm.1, ...), custom_call_target="tpu_custom_call" | custom-call | tf_op jit(solution)/shard_map/layer/pallas_call | solution.py:487
  106.5 3.0 %write_out.1 = (f32[64,4096]{1,0:T(8,128)}, f32[256,2048]{1,0:T(8,128)}, f32[512,2048]{1,0:T(8,128)}) custom-call(f32[64,4096]{1,0:T(8,128)S(1)} %get-tuple-element.6.att, f32[256,2048]{1,0:T(8,128)S(1)} %get-tuple-element.7.hid, f32[512,2048]{1,0:T(8,128)S(1)} %get-tuple-element.8.wg), custom_call_target="tpu_custom_call" | custom-call | tf_op jit(solution)/shard_map/write_out/pallas_call | solution.py:525

commit v7 on v6

--- a/solution.py
+++ b/solution.py
@@ -79,43 +79,43 @@
 
     def ux(j, k):
         block = u_rows(lax.rem(o - j + OUT, OUT), t)
-        return remote(block, block, send_sem.at[3], all_r.at[0], g,
+        return remote(block, block, send_sem.at[2], all_r.at[0], g,
                       lax.rem(x + k, XS) * 2 + core)
 
     def uc(j, k):
         block = u_rows(lax.rem(o - j + OUT, OUT), lax.rem(x - k + XS, XS) * 2 + core)
-        return remote(block, block, send_sem.at[4], all_r.at[1], g, x * 2 + 1 - core)
+        return remote(block, block, send_sem.at[2], all_r.at[1], g, x * 2 + 1 - core)
 
     def wx(c, j):
-        return remote(w_hbm.at[:, cols(c)], w_rows(c, i), send_sem.at[5], w_r.at[c],
+        return remote(w_hbm.at[:, cols(c)], w_rows(c, i), send_sem.at[3], w_r.at[c],
                       o * INN + lax.rem(i + j, INN), t)
 
     def a_right(c, s, n):
         block = a_rows(c, jnp.maximum(o - s, 0))
-        return remote(block, block, send_sem.at[0], z_r.at[0, n],
+        return remote(block, block, send_sem.at[0], z_r.at[n],
                       jnp.minimum(o + 1, OUT - 1) * INN + i, t)
 
     def a_left(c, s, n):
         block = a_rows(c, jnp.minimum(o + s, OUT - 1))
-        return remote(block, block, send_sem.at[1], z_r.at[1, n],
+        return remote(block, block, send_sem.at[1], z_r.at[n],
                       jnp.maximum(o - 1, 0) * INN + i, t)
 
     def h_r(c, e, n):
-        return remote(h_right.at[c, e], h_right.at[c, e], send_sem.at[0], z_r.at[0, n],
+        return remote(h_right.at[c, e], h_right.at[c, e], send_sem.at[0], z_r.at[n],
                       jnp.minimum(o + 1, OUT - 1) * INN + i, t)
 
     def h_l(c, e, n):
-        return remote(h_left.at[c, e], h_left.at[c, e], send_sem.at[1], z_r.at[1, n],
+        return remote(h_left.at[c, e], h_left.at[c, e], send_sem.at[1], z_r.at[n],
                       jnp.maximum(o - 1, 0) * INN + i, t)
 
     def gx(c, j):
-        return remote(g_send.at[c, j - 1], g_recv.at[c, j - 1], send_sem.at[6], all_r.at[3],
+        return remote(g_send.at[c, j - 1], g_recv.at[c, j - 1], send_sem.at[4], all_r.at[3],
                       o * INN + lax.rem(i + j, INN), t)
 
     def att(j):
         to = lax.rem(t + j, TEN)
         return remote(part.at[pl.ds(pl.multiple_of(to * rows, rows), rows), :],
-                      att_recv.at[j - 1], send_sem.at[7], all_r.at[2], g, to)
+                      att_recv.at[j - 1], send_sem.at[5], all_r.at[2], g, to)
 
     def own_w(c):
         return pltpu.make_async_copy(w_hbm.at[:, cols(c)], w_rows(c, i), local_sem.at[6])
@@ -210,16 +210,25 @@
     u_all[pl.ds(pl.multiple_of((o * TEN + t) * rows, rows), rows), :] = (
         up[:, pl.ds(pl.multiple_of(o * dcols, dcols), dcols)])
 
-    right = (o, lambda p: p, a_right, z_r.at[0], h_right, h_r)
-    left = (OUT - 1 - o, lambda p: OUT - 1 - p, a_left, z_r.at[1], h_left, h_l)
-
-    def a_wait(direction, c, s):
-        r, place, _, arrived, _, _ = direction
-        step = c // GROUP * GROUP * r + (s - 1) * GROUP + lax.rem(c, GROUP)
-        landed(a_rows(c, place(jnp.maximum(r - s, 0))), arrived.at[step])
+    right = (o, lambda p: p, a_right, h_right, h_r)
+    left = (OUT - 1 - o, lambda p: OUT - 1 - p, a_left, h_left, h_l)
+    steps = OUT * CHUNKS
+
+    def items(count):
+        return a_all.at[0, pl.ds(0, count * tokens), :]
+
+    def relayed(n):
+        used = 0
+        for r in (o, OUT - 1 - o):
+            own = (n < (r + 1) * CHUNKS) & (lax.rem(n, (r + 1) * GROUP) < GROUP)
+            used = used + jnp.where((r > 0) & (r < OUT - 1) & jnp.logical_not(own), 1, 0)
+        for count in (1, 2):
+            @pl.when(used == count)
+            def _():
+                landed(items(count), z_r.at[n])
 
     def a_item(direction, n):
-        r, _, copy, _, _, _ = direction
+        r, _, copy, _, _ = direction
         turn = (r + 1) * GROUP
         rest = lax.rem(n, turn)
         s = rest // GROUP
@@ -227,10 +236,8 @@
 
         @pl.when((r < OUT - 1) & (n < (r + 1) * CHUNKS))
         def _():
-            @pl.when(s > 0)
-            def _():
-                a_wait(direction, c, s)
-            copy(c, s, n).start()
+            later = n + (n // turn + 1) * GROUP
+            copy(c, s, jnp.where(r == OUT - 2, c, later)).start()
 
     def activate(c):
         act = gelu_exact(pre[:, cols(c)].astype(jnp.float32)).astype(jnp.bfloat16)
@@ -303,29 +310,28 @@
         return jnp.dot(u_all[span, :], w_all[c], preferred_element_type=jnp.float32)
 
     def h_item(direction, n):
-        r, place, _, arrived, held, copy = direction
+        r, place, _, held, copy = direction
         m = n - (r + 1) * CHUNKS
         e = place(OUT - 1 - m // CHUNKS)
         c = lax.rem(m, CHUNKS)
+        slot = n + CHUNKS
 
         @pl.when((m >= 0) & (r == 0))
         def _():
             held[c, e] = partial(c, e).astype(jnp.bfloat16)
-            copy(c, e, n).start()
+            copy(c, e, slot).start()
 
         @pl.when((m >= 0) & (r > 0) & (r < OUT - 1))
         def _():
             mine = partial(c, e)
-            landed(held.at[c, e], arrived.at[n - CHUNKS])
             held[c, e] = (mine + held[c, e].astype(jnp.float32)).astype(jnp.bfloat16)
-            copy(c, e, n).start()
+            copy(c, e, slot).start()
 
     def weight_chunk(c):
         for direction in (right, left):
             @pl.when(direction[0] == OUT - 1)
             def _():
-                for s in range(1, OUT):
-                    a_wait(direction, c, s)
+                landed(items(OUT - 1), z_r.at[c])
         for j in range(1, INN):
             to = lax.rem(i + j, INN)
             span = pl.ds(pl.multiple_of(to * rows_w, rows_w), rows_w)
@@ -349,6 +355,7 @@
     loop(early, project)
 
     def relay(n):
+        relayed(n)
         a_item(right, n)
         a_item(left, n)
 
@@ -373,6 +380,7 @@
         def _():
             landed(g_recv.at[first], w_r.at[first])
 
+        relayed(n)
         for direction in (right, left):
             a_item(direction, n)
             h_item(direction, n)
@@ -418,34 +426,29 @@
         wg_out[:, cols(c)] = acc * factor
 
     loop(CHUNKS, finish)
-    sent(up.at[:, pl.ds(0, (OUT - 1) * dcols)], 2)
-    if XS > 1:
-        sent(u_all.at[pl.ds(0, OUT * (XS - 1) * rows), :], 3)
-    sent(u_all.at[pl.ds(0, OUT * XS * rows), :], 4)
-    sent(g_send, 5)
-    sent(g_send, 6)
-    sent(att_recv, 7)
-    final = (OUT - 1) * CHUNKS
+    sent(u_all.at[pl.ds(0, (OUT * TEN - 1) * rows), :], 2)
+    sent(g_send, 3)
+    sent(g_send, 4)
+    sent(att_recv, 5)
 
     def close(c):
         slope = gelu_slope(pre[:, cols(c)].astype(jnp.float32))
 
         @pl.when(o == 0)
         def _():
-            landed(h_left.at[c, o], z_r.at[1, final + c])
+            landed(items(1), z_r.at[steps + c])
             hid_out[:, cols(c)] = (
                 hid_out[:, cols(c)] + h_left[c, o].astype(jnp.float32)) * slope
 
         @pl.when(o == OUT - 1)
         def _():
-            landed(h_right.at[c, o], z_r.at[0, final + c])
+            landed(items(1), z_r.at[steps + c])
             hid_out[:, cols(c)] = (
                 hid_out[:, cols(c)] + h_right[c, o].astype(jnp.float32)) * slope
 
         @pl.when((o > 0) & (o < OUT - 1))
         def _():
-            landed(h_right.at[c, o], z_r.at[0, final + c])
-            landed(h_left.at[c, o], z_r.at[1, final + c])
+            landed(items(2), z_r.at[steps + c])
             hid_out[:, cols(c)] = (
                 hid_out[:, cols(c)] + h_right[c, o].astype(jnp.float32)
                 + h_left[c, o].astype(jnp.float32)) * slope
@@ -512,7 +515,7 @@
             pltpu.VMEM((CHUNKS, OUT, tokens, fc), bf),
             pltpu.VMEM((CHUNKS, INN - 1, rows_w, fc), bf),
             pltpu.VMEM((CHUNKS, INN - 1, rows_w, fc), bf),
-            dma(7), dma(8), dma(2, OUT * CHUNKS), dma(OUT - 1), dma(CHUNKS), dma(4),
+            dma(7), dma(6), dma((OUT + 1) * CHUNKS), dma(OUT - 1), dma(CHUNKS), dma(4),
             pltpu.SemaphoreType.REGULAR((2,)),
         ],
         compiler_params=pltpu.CompilerParams(

time: 110 us -> 110 us (level)
  no operation moved by 1% of the time
where the time goes in v7:
time: 110 us; the launch traced here: 109 us
  Pallas kernels  109 us (99%)
    pallas_call x1, Pallas kernels, body(): pl.pallas_call(functools.partial(kernel, sizes), out_shape=(pltpu.VMEM((r...  106 us
    pallas_call x1, Pallas kernels, body(): pl.pallas_call(write_out, out_shape=tuple((jax.ShapeDtypeStruct(r.shape,...  3.01 us

profile of v7, /device:TPU:8, one launch (start us, length us, event | category | flops | bytes accessed | tf_op | source)
XLA Modules:
  0.0 109.4 jit_solution(3391002916437973399)
XLA Ops:
  0.6 105.8 %layer.1 = (f32[64,4096]{1,0:T(8,128)S(1)}, f32[256,2048]{1,0:T(8,128)S(1)}, f32[512,2048]{1,0:T(8,128)S(1)}) custom-call(bf16[3,256,1024]{2,1,0:T(8,128)(2,1)} %qkv_hbm.1, s32[1,4,64]{2,1,0:T(4,128)} %names_hbm.1, bf16[4096,1024]{1,0:T(8,128)(2,1)} %ow_hbm.1, bf16[4096]{0:T(1024)(128)(2,1)} %bias_hbm.1, bf16[64,4096]{1,0:T(8,128)(2,1)} %up_hbm.1, ...), custom_call_target="tpu_custom_call" | custom-call | tf_op jit(solution)/shard_map/layer/pallas_call | solution.py:490
  106.4 3.0 %write_out.1 = (f32[64,4096]{1,0:T(8,128)}, f32[256,2048]{1,0:T(8,128)}, f32[512,2048]{1,0:T(8,128)}) custom-call(f32[64,4096]{1,0:T(8,128)S(1)} %get-tuple-element.6.att, f32[256,2048]{1,0:T(8,128)S(1)} %get-tuple-element.7.hid, f32[512,2048]{1,0:T(8,128)S(1)} %get-tuple-element.8.wg), custom_call_target="tpu_custom_call" | custom-call | tf_op jit(solution)/shard_map/write_out/pallas_call | solution.py:528

commit v8 on v7

--- a/solution.py
+++ b/solution.py
@@ -146,8 +146,6 @@
         pl.semaphore_signal(semaphore, inc=1, device_id={"dp": dp, "tensor": tensor},
                             device_id_type=pl.DeviceIdType.MESH)
 
-    load_up.start()
-    load_pre.start()
     partners = (
         [(o * INN + lax.rem(i + j, INN), t) for j in range(1, INN)]
         + [(g, lax.rem(t + j, TEN)) for j in range(1, TEN)])
@@ -163,6 +161,8 @@
 
     for dp, tensor in partners:
         signal(barrier, dp, tensor)
+    load_up.start()
+    load_pre.start()
     load_up.wait()
     sides = jnp.minimum(o, 1) + jnp.minimum(OUT - 1 - o, 1)
     pl.semaphore_wait(barrier, len(partners) + sides)

time: 110 us -> 110 us (level)
  no operation moved by 1% of the time
where the time goes in v8:
time: 110 us; the launch traced here: 109 us
  Pallas kernels  109 us (99%)
    pallas_call x1, Pallas kernels, body(): pl.pallas_call(functools.partial(kernel, sizes), out_shape=(pltpu.VMEM((r...  106 us
    pallas_call x1, Pallas kernels, body(): pl.pallas_call(write_out, out_shape=tuple((jax.ShapeDtypeStruct(r.shape,...  3.01 us

profile of v8, /device:TPU:8, one launch (start us, length us, event | category | flops | bytes accessed | tf_op | source)
XLA Modules:
  0.0 109.4 jit_solution(17586024302991738804)
XLA Ops:
  0.6 105.8 %layer.1 = (f32[64,4096]{1,0:T(8,128)S(1)}, f32[256,2048]{1,0:T(8,128)S(1)}, f32[512,2048]{1,0:T(8,128)S(1)}) custom-call(bf16[3,256,1024]{2,1,0:T(8,128)(2,1)} %qkv_hbm.1, s32[1,4,64]{2,1,0:T(4,128)} %names_hbm.1, bf16[4096,1024]{1,0:T(8,128)(2,1)} %ow_hbm.1, bf16[4096]{0:T(1024)(128)(2,1)} %bias_hbm.1, bf16[64,4096]{1,0:T(8,128)(2,1)} %up_hbm.1, ...), custom_call_target="tpu_custom_call" | custom-call | tf_op jit(solution)/shard_map/layer/pallas_call | solution.py:490
  106.4 3.0 %write_out.1 = (f32[64,4096]{1,0:T(8,128)}, f32[256,2048]{1,0:T(8,128)}, f32[512,2048]{1,0:T(8,128)}) custom-call(f32[64,4096]{1,0:T(8,128)S(1)} %get-tuple-element.6.att, f32[256,2048]{1,0:T(8,128)S(1)} %get-tuple-element.7.hid, f32[512,2048]{1,0:T(8,128)S(1)} %get-tuple-element.8.wg), custom_call_target="tpu_custom_call" | custom-call | tf_op jit(solution)/shard_map/write_out/pallas_call | solution.py:528
